TPU v7x, 512 devices: a whole 4x8x8 slice. The times are simulated.
512 devices in a mesh: dp: 32 (over x, z), patch: 16 (over y, core).
Axes of the slice: x: 4, y: 8, z: 8, core: 2. Of those that a mesh axis runs over, the one named last changes fastest.
Arguments:
- query_rows: bfloat16 [32, 2048, 576], P('dp', 'patch'), may hold values from -6 to 6
- key_rows: bfloat16 [32, 2048, 576], P('dp', 'patch'), may hold values from -6 to 6
- value_rows: bfloat16 [32, 2048, 576], P('dp', 'patch'), may hold values from -6 to 6
- out_weight: bfloat16 [576, 1152], replicated, may hold values from -0.25 to 0.25
- target: bfloat16 [32, 2048, 1152], P('dp', 'patch'), may hold values from -6 to 6
- lengths: int32 [32], P('dp'), may hold values from 256 to 2048
- segments: int32 [32, 2048], P('dp', 'patch'), may hold values from 0 to 7, never falling along the last dimension, each value on 1 to 1024 neighbouring positions
Outputs:
- query_grad: float32 [32, 2048, 576], P('dp', 'patch')
- key_grad: float32 [32, 2048, 576], P('dp', 'patch')
- value_grad: float32 [32, 2048, 576], P('dp', 'patch')
- weight_grad: float32 [576, 1152], P('patch', 'dp')
- loss: float32 [], replicated
All inputs are finite; a program needn't handle non-finite values.
Results may differ from a plain program's by a relative error of at most 0.024.
Values may be sent and summed in bfloat16 or wider, within the bound.
A program may use at most 64 MiB of HBM per device.

v0:
```python
import math

import jax
import jax.numpy as jnp
from jax import lax
from jax.sharding import Mesh
from jax.sharding import PartitionSpec as P

WIDTH = 1152
HEADS = 8
HEAD_DIM = 72
FEAT = 576
PATCH = ("patch_0", "patch_1")
DP = ("dp_0", "dp_1")
DP_PATCH = ("dp_0", "dp_1", "patch_0", "patch_1")


NEG_LARGE = -1e30


def from_everyone(value, axis):
    copies = jnp.broadcast_to(value, (lax.axis_size(axis), *value.shape))
    return lax.all_to_all(copies, axis, split_axis=0, concat_axis=0, tiled=True)


def of_everyone(value, axis):
    return from_everyone(value, axis).sum(axis=0)


def sent_together(arrays, axis, dim, along):
    ends, at = ([], 0)
    for a in arrays[:-1]:
        at += a.shape[along]
        ends.append(at)
    both = jnp.concatenate(arrays, axis=along)
    return tuple(jnp.split(lax.all_gather(both, axis, axis=dim, tiled=True), ends, axis=along))


def by_axis(value, axes):
    for axis in axes:
        value = lax.psum(value, axis)
    return value


def in_blocks(value, dim, peers):
    shape = value.shape
    pieces = value.reshape(*shape[:dim], peers, shape[dim] // peers, *shape[dim + 1 :])
    return jnp.moveaxis(pieces, dim, 0)


def sum_at_owner(value, axis, dim):
    peers = lax.axis_size(axis)
    pieces = lax.all_to_all(in_blocks(value, dim, peers), axis, 0, 0, tiled=True)
    return jnp.sum(pieces.astype(jnp.float32), axis=0)


def head_view(rows):
    return rows.reshape(rows.shape[0], HEADS, HEAD_DIM)


def pair_mask(query_group, key_group):
    return (query_group[:, None] == key_group[None, :])[None, :, :]


def forward_block(running, query_heads, own_group, group_all, pieces):
    run_max, run_denom, run_accum = running
    score_scale = 1.0 / math.sqrt(HEAD_DIM)
    key_heads = head_view(pieces[0][0])
    value_heads = head_view(pieces[1][0])
    allowed = pair_mask(own_group, group_all)
    scores = (
        jnp.einsum("qhe,khe->hqk", query_heads, key_heads, preferred_element_type=jnp.float32)
        * score_scale
    )
    masked = jnp.where(allowed, scores, NEG_LARGE)
    new_max = jnp.maximum(run_max, jnp.max(masked, axis=2))
    probs = jnp.where(allowed, jnp.exp(masked - new_max[:, :, None]), 0.0)
    shrink = jnp.exp(run_max - new_max)
    run_denom = jnp.sum(probs, axis=2)
    added = jnp.einsum(
        "hqk,khe->qhe", probs.astype(jnp.bfloat16), value_heads, preferred_element_type=jnp.float32
    )
    run_accum = run_accum * shrink.T[:, :, None] + added
    return (new_max, run_denom, run_accum)


def query_grad_block(query_heads, grad_heads, log_norm, delta, own_group, group_all, pieces):
    score_scale = 1.0 / math.sqrt(HEAD_DIM)
    key_heads = head_view(pieces[0][0])
    value_heads = head_view(pieces[1][0])
    allowed = pair_mask(own_group, group_all)
    scores = (
        jnp.einsum("qhe,khe->hqk", query_heads, key_heads, preferred_element_type=jnp.float32)
        * score_scale
    )
    masked = jnp.where(allowed, scores, NEG_LARGE)
    probs = jnp.where(allowed, jnp.exp(masked - log_norm[:, :, None]), 0.0)
    dprobs = jnp.einsum("qhe,khe->hqk", grad_heads, value_heads, preferred_element_type=jnp.float32)
    dscores = (probs * (dprobs - delta[:, :, None])).astype(jnp.bfloat16)
    return (
        jnp.einsum("hqk,khe->qhe", dscores, key_heads, preferred_element_type=jnp.float32)
        * score_scale
    )


def key_grad_block(own_keys, own_values, own_group, group_all, log_all, delta_all, pieces):
    score_scale = 1.0 / math.sqrt(HEAD_DIM)
    query_heads = head_view(pieces[0][0])
    grad_heads = head_view(pieces[1][0])
    allowed = pair_mask(group_all, own_group)
    scores = (
        jnp.einsum("qhe,khe->hqk", query_heads, own_keys, preferred_element_type=jnp.float32)
        * score_scale
    )
    masked = jnp.where(allowed, scores, NEG_LARGE)
    probs = jnp.where(allowed, jnp.exp(masked - log_all[:, :, None]), 0.0)
    grad_values = jnp.einsum(
        "hqk,qhe->khe", probs.astype(jnp.bfloat16), grad_heads, preferred_element_type=jnp.float32
    )
    dprobs = jnp.einsum("qhe,khe->hqk", grad_heads, own_values, preferred_element_type=jnp.float32)
    dscores = (probs * (dprobs - delta_all[:, :, None])).astype(jnp.bfloat16)
    grad_keys = (
        jnp.einsum("hqk,qhe->khe", dscores, query_heads, preferred_element_type=jnp.float32)
        * score_scale
    )
    return (grad_keys, grad_values)


def local(query_rows, key_rows, value_rows, out_weight, target, lengths, segments):
    own_rows = query_rows.shape[1]
    members = lax.axis_size(PATCH)
    groups = lax.axis_size(DP)
    total_rows = own_rows * members
    length = lengths[0]
    count = of_everyone(length.astype(jnp.float32), DP)
    offset = lax.axis_index(PATCH) * own_rows
    own_live = offset + lax.iota(jnp.int32, own_rows) < length
    segment_all = lax.all_gather(segments, PATCH, axis=1, tiled=True)
    group_all = jnp.where(lax.iota(jnp.int32, total_rows) < length, segment_all[0], -1)
    own_group = lax.dynamic_slice_in_dim(group_all, offset, own_rows, 0)
    query_heads = head_view(query_rows[0])
    starting = (
        jnp.full((HEADS, own_rows), NEG_LARGE, jnp.float32),
        jnp.zeros((HEADS, own_rows), jnp.float32),
        jnp.zeros((own_rows, HEADS, HEAD_DIM), jnp.float32),
    )
    forward_state = forward_block(
        starting,
        query_heads,
        own_group,
        group_all,
        sent_together((key_rows, value_rows), PATCH, 1, 0),
    )
    run_max, run_denom, run_accum = forward_state
    log_norm = run_max + jnp.log(run_denom)
    attn = (run_accum / run_denom.T[:, :, None]).reshape(own_rows, FEAT).astype(jnp.bfloat16)
    output = jnp.dot(attn, out_weight, preferred_element_type=jnp.float32)
    error = jnp.where(own_live[:, None], output - target[0].astype(jnp.float32), 0.0)
    loss_part = jnp.sum(error * error)
    grad_out = (2.0 * error).astype(jnp.bfloat16)
    weight_part = jnp.einsum("tf,td->fd", attn, grad_out, preferred_element_type=jnp.float32)
    grad_attn = jnp.einsum(
        "td,fd->tf", grad_out, out_weight, preferred_element_type=jnp.float32
    ).astype(jnp.bfloat16)
    delta = jnp.sum(
        (grad_attn.astype(jnp.float32) * attn.astype(jnp.float32)).reshape(
            own_rows, HEADS, HEAD_DIM
        ),
        axis=2,
    ).T
    grad_heads = head_view(grad_attn)
    query_raw = query_grad_block(
        query_heads,
        grad_heads,
        log_norm,
        delta,
        own_group,
        group_all,
        sent_together((key_rows, value_rows), PATCH, 1, 0),
    )
    log_all, delta_all = sent_together((log_norm, delta), PATCH, 1, 0)
    own_keys = head_view(key_rows[0])
    own_values = head_view(value_rows[0])
    key_raw, value_raw = key_grad_block(
        own_keys,
        own_values,
        own_group,
        group_all,
        log_all,
        delta_all,
        sent_together((query_rows, grad_attn[None]), PATCH, 1, 0),
    )
    loss_total = by_axis(loss_part, DP_PATCH)
    row_share = sum_at_owner(weight_part.astype(jnp.bfloat16), PATCH, 0)
    weight_share = sum_at_owner(row_share.astype(jnp.bfloat16), DP, 1)
    ratio = jnp.float32(groups * total_rows) / count
    query_grad = (ratio * query_raw).reshape(1, own_rows, FEAT)
    key_grad = (ratio * key_raw).reshape(1, own_rows, FEAT)
    value_grad = (ratio * value_raw).reshape(1, own_rows, FEAT)
    weight_grad = weight_share * (ratio / total_rows)
    loss = loss_total / (count * WIDTH)
    return (query_grad, key_grad, value_grad, weight_grad, loss)


def solution(mesh):
    torus = Mesh(mesh.devices.reshape(4, 8, 8, 2), ("dp_0", "dp_1", "patch_0", "patch_1"))
    return jax.shard_map(
        local,
        mesh=torus,
        in_specs=(
            P(DP, PATCH, None),
            P(DP, PATCH, None),
            P(DP, PATCH, None),
            P(),
            P(DP, PATCH, None),
            P(DP),
            P(DP, PATCH),
        ),
        out_specs=(P(DP, PATCH, None), P(DP, PATCH, None), P(DP, PATCH, None), P(PATCH, DP), P()),
        check_vma=False,
    )
```

profile of v0, /device:TPU:1, one launch (start us, length us, event | category | flops | bytes accessed | tf_op | source)
XLA Modules:
  0.0 233.7 jit_solution(14534418018708874223)
XLA Ops:
  7.2 0.0 copy-start
  7.2 0.0 copy-start.9
  7.2 0.0 all-gather.3.cloned.1.call-start
  7.2 1.8 pad_maximum_fusion
  9.1 0.0 all-gather.3.cloned.1.call-update
  9.1 0.0 all-gather.5.cloned.1.call-start
  9.8 21.1 %all_gather.14 = s32[1,2048]{1,0:T(1,128)S(1)} all-gather(s32[1,128]{1,0:T(1,128)} %param.13), channel_id=1, replica_groups=mesh['dp_0'=4,'dp_1'=8,'patch_0'=8,'patch_1'=2] {'patch_0','patch_1'}, dimensions={1}, use_global_device_ids=true | all-gather | bytes 8704 | tf_op jit(solution)/shard_map/all_gather | solution.py:138
  30.9 0.1 dynamic_slice.3
  31.0 0.3 broadcast_compare_fusion.1
  31.3 40.1 %all-gather.3.cloned.1.call-done = bf16[2,2048,576]{1,2,0:T(8,128)(2,1)} async-done(((bf16[2,128,576]{1,2,0:T(8,128)(2,1)}), bf16[2,2048,576]{1,2,0:T(8,128)(2,1)}) %all-gather.3.cloned.1.call-update) | async-done | bytes 4718608 | tf_op jit(solution)/shard_map/all_gather | solution.py:36
  71.4 2.8 %fusion.46 = (bf16[1,2048,576]{1,2,0:T(8,128)(2,1)S(1)}, bf16[1,2048,576]{1,2,0:T(8,128)(2,1)S(1)}) fusion(bf16[2,2048,576]{1,2,0:T(8,128)(2,1)} %all-gather.3.cloned.1.call-done), kind=kLoop, calls=%fused_computation.58 | loop fusion | bytes 9437184 | tf_op jit(solution)/shard_map/split | solution.py:36
  74.1 0.0 copy-start.2
  74.1 0.0 copy-start.5
  74.1 0.0 copy-done.9
  74.2 2.2 fusion.3
  76.3 0.0 copy-start.1
  76.3 2.0 fusion.1
  78.4 0.0 copy-done.2
  78.4 0.0 copy-done.5
  78.4 0.0 copy-start.11
  78.4 2.9 %fusion.27 = bf16[128,8,72]{0,2,1:T(8,128)(2,1)S(1)} fusion(bf16[2048,8,72]{0,2,1:T(8,128)(2,1)S(1)} %bitcast.87, f32[8,2048,128]{2,1,0:T(8,128)S(1)} %get-tuple-element.14, f32[8,128]{1,0:T(8,128)S(1)} %broadcast_maximum_fusion, pred[128,2048]{0,1:T(8,128)(4,1)S(1)} %broadcast_compare_fusion.1, f32[128,8]{0,1:T(8,128)S(1)} %bitcast.102, ...), kind=kOutput, calls=%fused_computation.25 | convolution fusion | flops 312696832 | bytes 11169792 | tf_op jit(solution)/shard_map/hqk,khe->qhe/dot_general | solution.py:80
  81.3 0.0 copy-done.1
  81.4 0.0 copy-start.7
  81.4 0.0 copy-done
  81.4 0.0 copy-done.11
  81.4 1.1 multiply_reduce_fusion
  82.5 1.2 convert_multiply_fusion
  83.7 0.8 pad_maximum_fusion.1
  84.5 0.0 all-gather.5.cloned.1.call-update
  84.5 0.6 broadcast_in_dim.100
  85.1 0.0 copy-done.7
  85.1 0.0 copy-done.8
  85.1 8.3 %all-to-all-start = ((f32[32,1,1]{2,1,0:T(1,128)}), f32[32,1,1]{2,1,0:T(1,128)S(1)}, u32[]{:S(2)}, u32[]{:S(2)}) async-start(f32[32,1,1]{2,1,0:T(1,128)} %broadcast_in_dim.100), calls=%async_computation | async-start | bytes 32768 | tf_op jit(solution)/shard_map/all_to_all | solution.py:23
  93.4 1.4 convolution_convert_fusion
  94.8 1.3 reshape.133
  96.1 5.9 %all-to-all-done = f32[32,1,1]{2,1,0:T(1,128)S(1)} async-done(((f32[32,1,1]{2,1,0:T(1,128)}), f32[32,1,1]{2,1,0:T(1,128)S(1)}, u32[]{:S(2)}, u32[]{:S(2)}) %all-to-all-start) | async-done | bytes 160 | tf_op jit(solution)/shard_map/all_to_all | solution.py:23
  102.0 6.7 %all-to-all-start.1 = ((bf16[16,36,1152]{2,1,0:T(8,128)(2,1)}), bf16[16,36,1152]{2,1,0:T(8,128)(2,1)S(1)}, u32[]{:S(2)}, u32[]{:S(2)}) async-start(bf16[16,36,1152]{2,1,0:T(8,128)(2,1)} %reshape.133), calls=%async_computation.1 | async-start | bytes 2949120 | tf_op jit(solution)/shard_map/all_to_all | solution.py:53
  108.8 1.0 broadcast_compare_fusion
  109.8 0.6 reduce_sum.59
  111.1 8.2 %psum.28 = f32[]{:T(128)} all-reduce(f32[]{:T(128)} %get-tuple-element.17), channel_id=1, replica_groups=mesh['dp_0'=4,'dp_1'=8,'patch_0'=8,'patch_1'=2] {'dp_0'}, use_global_device_ids=true, to_apply=%region_7.8 | all-reduce | flops 1 | bytes 8 | tf_op jit(solution)/shard_map/psum | solution.py:41
  119.3 13.3 %psum.29 = f32[]{:T(128)} all-reduce(f32[]{:T(128)} %psum.28), channel_id=1, replica_groups=mesh['dp_0'=4,'dp_1'=8,'patch_0'=8,'patch_1'=2] {'dp_1'}, use_global_device_ids=true, to_apply=%region_8.9 | all-reduce | flops 1 | bytes 8 | tf_op jit(solution)/shard_map/psum | solution.py:41
  133.3 30.3 %psum.30 = f32[]{:T(128)} all-reduce(f32[]{:T(128)} %psum.29), channel_id=1, replica_groups=mesh['dp_0'=4,'dp_1'=8,'patch_0'=8,'patch_1'=2] {'patch_0'}, use_global_device_ids=true, to_apply=%region_9.10 | all-reduce | flops 1 | bytes 8 | tf_op jit(solution)/shard_map/psum | solution.py:41
  163.6 1.0 reduce_sum.58
  164.6 17.3 %all_gather.16 = f32[16,2048]{1,0:T(8,128)S(1)} all-gather(f32[16,128]{1,0:T(8,128)S(1)} %pad_maximum_fusion.2), channel_id=1, replica_groups=mesh['dp_0'=4,'dp_1'=8,'patch_0'=8,'patch_1'=2] {'patch_0','patch_1'}, dimensions={1}, use_global_device_ids=true | all-gather | bytes 139264 | tf_op jit(solution)/shard_map/all_gather | solution.py:36
  182.0 9.7 %fusion.20 = f32[8,72,128]{2,1,0:T(8,128)} fusion(bf16[2048,8,72]{0,2,1:T(8,128)(2,1)} %bitcast.84, f32[8,2048,128]{2,1,0:T(8,128)} %copy-done.1, bf16[128,8,72]{0,2,1:T(8,128)(2,1)} %bitcast.96, bf16[2048,8,72]{0,2,1:T(8,128)(2,1)} %bitcast.88, f32[8,128]{1,0:T(8,128)S(1)} %bitcast.104, f32[8,128]{1,0:T(8,128)S(1)} %get-tuple-element.11, ...), kind=kOutput, calls=%fused_computation.21 | convolution fusion | flops 618733568 | bytes 13819908 | tf_op jit(solution)/shard_map/hqk,khe->qhe/dot_general | solution.py:101
  191.7 0.0 all-to-all-done.1
  191.7 0.2 reduce_sum.60
  192.0 0.8 reshape.134
  192.8 0.1 copy.31
  192.9 1.0 reshape.136
  193.9 3.9 %all-to-all-start.2 = ((bf16[32,2,648]{2,1,0:T(2,128)(2,1)}), bf16[32,2,648]{2,1,0:T(2,128)(2,1)S(1)}, u32[]{:S(2)}, u32[]{:S(2)}) async-start(bf16[32,2,648]{2,1,0:T(2,128)(2,1)} %reshape.136), calls=%async_computation.2 | async-start | bytes 196608 | tf_op jit(solution)/shard_map/all_to_all | solution.py:53
  197.8 3.3 %psum.31 = f32[]{:T(128)} all-reduce(f32[]{:T(128)} %psum.30), channel_id=1, replica_groups=mesh['dp_0'=4,'dp_1'=8,'patch_0'=8,'patch_1'=2] {'patch_1'}, use_global_device_ids=true, to_apply=%region_10.11 | all-reduce | flops 1 | bytes 8 | tf_op jit(solution)/shard_map/psum | solution.py:41
  201.8 5.0 %all-to-all-done.2 = bf16[32,2,648]{2,1,0:T(2,128)(2,1)S(1)} async-done(((bf16[32,2,648]{2,1,0:T(2,128)(2,1)}), bf16[32,2,648]{2,1,0:T(2,128)(2,1)S(1)}, u32[]{:S(2)}, u32[]{:S(2)}) %all-to-all-start.2) | async-done | bytes 82976 | tf_op jit(solution)/shard_map/all_to_all | solution.py:53
  206.8 0.4 reshape.137
  207.2 0.1 convert_reduce_fusion
  207.3 0.6 broadcast_multiply_fusion
  207.9 2.8 %fusion.45 = (bf16[1,2048,576]{1,2,0:T(8,128)(2,1)S(1)}, bf16[1,2048,576]{1,2,0:T(8,128)(2,1)S(1)}) fusion(bf16[2,2048,576]{1,2,0:T(8,128)(2,1)} %all-gather.5.cloned.1.call-done), kind=kLoop, calls=%fused_computation.57 | loop fusion | bytes 9437184 | tf_op jit(solution)/shard_map/split | solution.py:36
  210.7 1.5 fusion.48
  212.2 0.0 copy-start.4
  212.2 0.0 copy-done.12
  212.2 0.0 copy-start.13
  212.2 3.9 %fusion.21 = f32[8,72,128]{2,1,0:T(8,128)} fusion(bf16[2048,8,72]{0,2,1:T(8,128)(2,1)S(1)} %bitcast.89, f32[8,2048,128]{2,1,0:T(8,128)S(1)} %fusion.48, f32[8,2048]{1,0:T(8,128)S(1)} %get-tuple-element.9, pred[2048,128]{1,0:T(8,128)(4,1)S(1)} %copy-done.12, f32[]{:T(128)S(6)} %div.19), kind=kOutput, calls=%fused_computation.22 | convolution fusion | flops 312549376 | bytes 11370500 | tf_op jit(solution)/shard_map/hqk,qhe->khe/dot_general | solution.py:117
  216.1 0.0 copy-done.13
  216.1 9.6 %fusion.19 = f32[8,72,128]{2,1,0:T(8,128)} fusion(bf16[2048,8,72]{0,2,1:T(8,128)(2,1)} %bitcast.86, f32[8,2048,128]{2,1,0:T(8,128)} %copy-done.4, bf16[2048,8,72]{0,2,1:T(8,128)(2,1)} %bitcast.90, bf16[128,8,72]{0,2,1:T(8,128)(2,1)S(1)} %bitcast.99, f32[8,2048]{1,0:T(8,128)S(1)} %get-tuple-element.10, f32[8,2048]{1,0:T(8,128)S(1)} %get-tuple-element.9, ...), kind=kOutput, calls=%fused_computation.20 | convolution fusion | flops 618733568 | bytes 13942788 | tf_op jit(solution)/shard_map/hqk,qhe->khe/dot_general | solution.py:123
  (17 shorter events, 0.1 us)
Async XLA Ops:
  7.2 74.2 %copy-start = (bf16[576,1152]{1,0:T(8,128)(2,1)S(1)}, bf16[576,1152]{1,0:T(8,128)(2,1)}, u32[]{:S(2)}) copy-start(bf16[576,1152]{1,0:T(8,128)(2,1)} %param.10) | copy-start | bytes 3981316
  7.2 67.0 %copy-start.9 = (bf16[1,128,576]{1,2,0:T(8,128)(2,1)S(1)}, bf16[1,128,576]{1,2,0:T(8,128)(2,1)}, u32[]{:S(2)}) copy-start(bf16[1,128,576]{1,2,0:T(8,128)(2,1)} %param.7) | copy-start | bytes 442372
  7.2 64.2 %all-gather.3.cloned.1.call-start = ((), (), s32[]{:S(2)}) async-start(), calls=%async_computation.3 | async-start | bytes 5013504 | tf_op jit(solution)/shard_map/all_gather | solution.py:36
  9.1 198.8 %all-gather.5.cloned.1.call-start = ((), (), s32[]{:S(2)}) async-start(), calls=%async_computation.4 | async-start | bytes 5013504 | tf_op jit(solution)/shard_map/all_gather | solution.py:36
  74.1 4.3 %copy-start.2 = (bf16[1,2048,576]{1,2,0:T(8,128)(2,1)}, bf16[1,2048,576]{1,2,0:T(8,128)(2,1)S(1)}, u32[]{:S(2)}) copy-start(bf16[1,2048,576]{1,2,0:T(8,128)(2,1)S(1)} %get-tuple-element.8) | copy-start | bytes 7077892
  74.1 4.3 %copy-start.5 = (bf16[1,2048,576]{1,2,0:T(8,128)(2,1)}, bf16[1,2048,576]{1,2,0:T(8,128)(2,1)S(1)}, u32[]{:S(2)}) copy-start(bf16[1,2048,576]{1,2,0:T(8,128)(2,1)S(1)} %get-tuple-element.7) | copy-start | bytes 7077892
  76.3 5.0 %copy-start.1 = (f32[8,2048,128]{2,1,0:T(8,128)}, f32[8,2048,128]{2,1,0:T(8,128)S(1)}, u32[]{:S(2)}) copy-start(f32[8,2048,128]{2,1,0:T(8,128)S(1)} %get-tuple-element.14) | copy-start | bytes 25165828
  78.4 3.0 %copy-start.11 = (bf16[1,128,1152]{2,1,0:T(8,128)(2,1)S(1)}, bf16[1,128,1152]{2,1,0:T(8,128)(2,1)}, u32[]{:S(2)}) copy-start(bf16[1,128,1152]{2,1,0:T(8,128)(2,1)} %param.11) | copy-start | bytes 884740
  81.4 3.8 %copy-start.7 = (bf16[128,8,72]{0,2,1:T(8,128)(2,1)}, bf16[128,8,72]{0,2,1:T(8,128)(2,1)S(1)}, u32[]{:S(2)}) copy-start(bf16[128,8,72]{0,2,1:T(8,128)(2,1)S(1)} %fusion.27) | copy-start | bytes 442372
  83.7 1.4 copy-start.8
  85.1 16.9 %all-to-all-start = ((f32[32,1,1]{2,1,0:T(1,128)}), f32[32,1,1]{2,1,0:T(1,128)S(1)}, u32[]{:S(2)}, u32[]{:S(2)}) async-start(f32[32,1,1]{2,1,0:T(1,128)} %broadcast_in_dim.100), calls=%async_computation | async-start | bytes 32768 | tf_op jit(solution)/shard_map/all_to_all | solution.py:23
  102.0 89.7 %all-to-all-start.1 = ((bf16[16,36,1152]{2,1,0:T(8,128)(2,1)}), bf16[16,36,1152]{2,1,0:T(8,128)(2,1)S(1)}, u32[]{:S(2)}, u32[]{:S(2)}) async-start(bf16[16,36,1152]{2,1,0:T(8,128)(2,1)} %reshape.133), calls=%async_computation.1 | async-start | bytes 2949120 | tf_op jit(solution)/shard_map/all_to_all | solution.py:53
  191.7 19.0 %copy-start.10 = (bf16[1,128,576]{1,2,0:T(8,128)(2,1)S(1)}, bf16[1,128,576]{1,2,0:T(8,128)(2,1)}, u32[]{:S(2)}) copy-start(bf16[1,128,576]{1,2,0:T(8,128)(2,1)} %param.8) | copy-start | bytes 442372
  193.9 12.9 %all-to-all-start.2 = ((bf16[32,2,648]{2,1,0:T(2,128)(2,1)}), bf16[32,2,648]{2,1,0:T(2,128)(2,1)S(1)}, u32[]{:S(2)}, u32[]{:S(2)}) async-start(bf16[32,2,648]{2,1,0:T(2,128)(2,1)} %reshape.136), calls=%async_computation.2 | async-start | bytes 196608 | tf_op jit(solution)/shard_map/all_to_all | solution.py:53
  207.9 4.3 %copy-start.12 = (pred[2048,128]{1,0:T(8,128)(4,1)S(1)}, pred[2048,128]{1,0:T(8,128)(4,1)}, u32[]{:S(2)}) copy-start(pred[2048,128]{1,0:T(8,128)(4,1)} %broadcast_compare_fusion) | copy-start | bytes 786436
  210.7 5.4 %copy-start.3 = (bf16[1,2048,576]{1,2,0:T(8,128)(2,1)}, bf16[1,2048,576]{1,2,0:T(8,128)(2,1)S(1)}, u32[]{:S(2)}) copy-start(bf16[1,2048,576]{1,2,0:T(8,128)(2,1)S(1)} %get-tuple-element.6) | copy-start | bytes 7077892
  210.7 5.4 %copy-start.6 = (bf16[1,2048,576]{1,2,0:T(8,128)(2,1)}, bf16[1,2048,576]{1,2,0:T(8,128)(2,1)S(1)}, u32[]{:S(2)}) copy-start(bf16[1,2048,576]{1,2,0:T(8,128)(2,1)S(1)} %get-tuple-element.5) | copy-start | bytes 7077892
  212.2 3.9 %copy-start.4 = (f32[8,2048,128]{2,1,0:T(8,128)}, f32[8,2048,128]{2,1,0:T(8,128)S(1)}, u32[]{:S(2)}) copy-start(f32[8,2048,128]{2,1,0:T(8,128)S(1)} %fusion.48) | copy-start | bytes 25165828
  212.2 3.9 %copy-start.13 = (bf16[1,128,576]{1,2,0:T(8,128)(2,1)S(1)}, bf16[1,128,576]{1,2,0:T(8,128)(2,1)}, u32[]{:S(2)}) copy-start(bf16[1,128,576]{1,2,0:T(8,128)(2,1)} %param.9) | copy-start | bytes 442372
Sparse Core Ops, SparseCore 0:
  10.6 60.7 all-gather.2
  84.6 78.2 all-gather.4
where the time goes:
time: 235 us; the launch traced here: 234 us
  blocking collectives  93.6 us (40%)
  waiting for transfers between devices  51 us (22%)
  matrix products  33.5 us (14%)
  starting transfers between devices  19 us (8%)
  between operations  18.1 us (8%)
  local copies, waits for them, and re-layouts  9.96 us (4%)
  other arithmetic  8.61 us (4%)
    psum x4, blocking collectives, by_axis(): value = lax.psum(value, axis)  55.2 us
    all_gather x2, waiting for transfers between devices, sent_together(): lax.all_gather(both, axis, axis=dim, tiled=True)  40.1 us
    all_gather x1, blocking collectives, local(): segment_all = lax.all_gather(segments, PATCH, axis=1, tiled=True)  21.1 us
    all_gather x1, blocking collectives, sent_together(): lax.all_gather(both, axis, axis=dim, tiled=True)  17.3 us
    all_to_all x2, starting transfers between devices, sum_at_owner(): lax.all_to_all(in_blocks(value, dim, peers), axis, 0, 0, tiled=True)  10.6 us
    dot_general x1, matrix products, query_grad_block(): jnp.einsum('hqk,khe->qhe', dscores, key_heads, preferred_element_type=jnp...  9.73 us
    dot_general x1, matrix products, key_grad_block(): jnp.einsum('hqk,qhe->khe', dscores, query_heads, preferred_element_type=j...  9.62 us
    all_to_all x1, starting transfers between devices, from_everyone(): return lax.all_to_all(copies, axis, split_axis=0, concat_axis=0, tiled=True)  8.3 us
  transfers between devices with their start and end apart: 5, of which 3 were waited for; matrix products, arithmetic and copies ran while one was open for 8% of the time, Pallas kernels for 0%

commit v1 on v0

v1 whole, which is shorter than its diff:
```python
import functools
import math

import jax
import jax.numpy as jnp
from jax import lax
from jax.experimental import pallas as pl
from jax.experimental.pallas import tpu as pltpu
from jax.sharding import Mesh
from jax.sharding import PartitionSpec as P

WIDTH = 1152
HEADS = 8
HEAD_DIM = 72
FEAT = 576
ROWS = 128
PAD = 80
PATCH = ("patch_0", "patch_1")
DP = ("dp_0", "dp_1")
BF = jnp.bfloat16
F32 = jnp.float32
FAR = (4, 3, 5, 2, 6, 1, 7)
MASK = 2.0**50


def dot(a, b, ca, cb):
    return lax.dot_general(a, b, (((ca,), (cb,)), ((), ())), preferred_element_type=F32)


def body(
    nx,
    nz,
    q_ref,
    k_ref,
    v_ref,
    seg_ref,
    len_ref,
    w_hbm,
    t_hbm,
    dq_out,
    dk_out,
    dv_out,
    wg_out,
    st_out,
    w_s,
    t_s,
    send1,
    recv1,
    ktok,
    vtok,
    qtok,
    dtok,
    p_s,
    ds_s,
    rinv_s,
    send2,
    recv2,
    at_s,
    send3,
    recv3,
    dof_s,
    dkv,
    drecv,
    send4,
    recv4,
    g_s,
    pg_s,
    pa_s,
    xsend,
    xrecv,
    zsend,
    zrecv,
    ysend,
    yrecv,
    stat_s,
    load_sem,
    s1,
    r1,
    d1s,
    d1r,
    s2,
    r2,
    s3,
    r3,
    dks,
    dkr,
    s4,
    r4,
    gs,
    gr,
    xs,
    xr,
    zs,
    zr,
    ys,
    yr,
    sts,
    strr,
):
    x = lax.axis_index("dp_0")
    z = lax.axis_index("dp_1")
    y = lax.axis_index("patch_0")
    k = lax.axis_index("patch_1")
    other = 1 - k
    p = 2 * y + k
    zh = nz // 2
    scale = 1.0 / math.sqrt(HEAD_DIM)

    load_w = pltpu.make_async_copy(w_hbm, w_s, load_sem.at[0])
    load_t = pltpu.make_async_copy(t_hbm, t_s, load_sem.at[1])
    load_w.start()
    load_t.start()

    barrier = pltpu.get_barrier_semaphore()
    for i in range(1, 8):
        peer = lax.rem(y + i, 8)
        pl.semaphore_signal(barrier, inc=1, device_id={"patch_0": peer})
        pl.semaphore_signal(barrier, inc=1, device_id={"patch_0": peer, "patch_1": other})
    pl.semaphore_signal(barrier, inc=1, device_id={"patch_1": other})
    for i in range(1, nx):
        pl.semaphore_signal(barrier, inc=1, device_id={"dp_0": lax.rem(x + i, nx)})
    for i in range(1, nz):
        pl.semaphore_signal(barrier, inc=1, device_id={"dp_1": lax.rem(z + i, nz)})

    def remote(src, dst, ssem, rsem, **where):
        return pltpu.make_async_remote_copy(
            src_ref=src, dst_ref=dst, send_sem=ssem, recv_sem=rsem, device_id=where
        )

    row = lax.broadcasted_iota(jnp.int32, (8, ROWS), 0)
    lane = lax.broadcasted_iota(jnp.int32, (8, ROWS), 1)
    length = len_ref[0]
    live_t = p * ROWS + lane < length
    code = jnp.where(live_t, jnp.broadcast_to(seg_ref[...], (8, ROWS)), 8)
    low = jnp.bitwise_and(row, 3)
    weight = jnp.where(low == 0, 1, jnp.where(low == 1, 2, jnp.where(low == 2, 4, 8)))
    bit = jnp.where(jnp.bitwise_and(code, weight) != 0, 1.0, 0.0).astype(F32)
    mine = jnp.where(row < 4, bit, 1.0 - bit)
    q_mask = -MASK * mine
    k_mask = MASK * (1.0 - mine)
    v_ones = jnp.where(row == 0, 1.0, 0.0).astype(F32)
    for at, (ref, extra) in enumerate(((q_ref, q_mask), (k_ref, k_mask), (v_ref, v_ones))):
        whole = ref[0].astype(F32).T
        for h in range(HEADS):
            block = jnp.concatenate([whole[HEAD_DIM * h : HEAD_DIM * (h + 1)], extra], axis=0)
            send1[h, PAD * at : PAD * (at + 1), :] = block.astype(BF)
    recv1[p] = send1[y]

    pl.semaphore_wait(barrier, 15 + (nx - 1) + (nz - 1))

    first = [None] * 8
    for i in FAR:
        h = lax.rem(y + i, 8)
        first[i] = remote(send1.at[h], recv1.at[p], s1.at[i], r1.at[i], patch_0=h)
        first[i].start()
    kv = pl.ds(PAD, 2 * PAD)

    def pass_on(i):
        b = 2 * lax.rem(y - i + 8, 8) + k
        return remote(
            recv1.at[b, kv], recv1.at[b, kv], d1s.at[i], d1r.at[i], patch_1=other
        )

    def prepare(b):
        at = pl.ds(pl.multiple_of(b * ROWS, ROWS), ROWS)
        both = recv1[b, PAD : 3 * PAD, :].astype(F32)
        ktok[at, :] = both[:PAD].T.astype(BF)
        vtok[at, :] = both[PAD:].T.astype(BF)

    def prepare_q(src):
        at = pl.ds(pl.multiple_of(src * ROWS, ROWS), ROWS)
        qtok[at, :] = recv1[2 * src + k, 0:PAD, :].astype(F32).T.astype(BF)

    passed = [pass_on(i) for i in range(8)]
    passed[0].start()
    prepare(p)
    prepare_q(y)
    for i in (1, 7, 2, 6, 3, 5, 4):
        first[i].wait_recv()
        passed[i].start()
        src = lax.rem(y - i + 8, 8)
        prepare(2 * src + k)
        prepare_q(src)
    for i in (0, 1, 7, 2, 6, 3, 5, 4):
        passed[i].wait_recv()
        prepare(2 * lax.rem(y - i + 8, 8) + other)

    factor = scale * math.log2(math.e)

    def queries(j, part):
        return jnp.concatenate(
            [recv1[4 * j + k, part, :], recv1[4 * j + 2 + k, part, :]], axis=1
        )

    def forward(j, carry):
        scores = dot(ktok[...], queries(j, slice(0, PAD)), 1, 0)
        top = jnp.max(scores, axis=0, keepdims=True)
        probs = jnp.exp2((scores - top) * factor).astype(BF)
        p_s[j] = probs
        values = jnp.concatenate([recv1[b, 2 * PAD : 3 * PAD, :] for b in range(16)], axis=1)
        accum = dot(values, probs, 1, 0)
        rinv = 1.0 / accum[HEAD_DIM : HEAD_DIM + 1, :]
        rinv_s[j] = jnp.broadcast_to(rinv, (8, 2 * ROWS))
        attn = (accum * rinv).astype(BF)
        send2[2 * j] = attn[:, :ROWS]
        send2[2 * j + 1] = attn[:, ROWS:]
        return carry

    lax.fori_loop(0, 4, forward, 0)
    second = [None] * 8
    for i in FAR:
        to = lax.rem(y + i, 8)
        second[i] = remote(send2.at[to], recv2.at[y], s2.at[i], r2.at[i], patch_0=to)
        second[i].start()
    recv2[y] = send2[y]

    load_w.wait()
    load_t.wait()
    for i in (1, 7, 2, 6, 3, 5, 4):
        second[i].wait_recv()
    for h in range(HEADS):
        at_s[HEAD_DIM * h : HEAD_DIM * (h + 1), :] = recv2[h].astype(F32)[:HEAD_DIM]
    attn_t = at_s[...].astype(BF)
    pa_s[0] = attn_t
    output = dot(attn_t, w_s[...], 0, 0)
    token = lax.broadcasted_iota(jnp.int32, (ROWS, WIDTH), 0)
    live = p * ROWS + token < length
    error = jnp.where(live, output - t_s[0].astype(F32), 0.0)
    grad_out = (2.0 * error).astype(BF)
    grad_attn = dot(w_s[...], grad_out, 1, 1)
    for h in range(HEADS):
        block = jnp.concatenate(
            [grad_attn[HEAD_DIM * h : HEAD_DIM * (h + 1)], jnp.zeros((8, ROWS), F32)], axis=0
        )
        send3[h] = block.astype(BF)
    third = [None] * 8
    for i in FAR:
        to = lax.rem(y + i, 8)
        third[i] = remote(send3.at[to], recv3.at[y], s3.at[i], r3.at[i], patch_0=to)
        third[i].start()
    recv3[y] = send3[y]

    grad_t = (2.0 * error).T.astype(BF)
    part = WIDTH // (2 * nx)
    for half in range(2):
        for xx in range(nx):
            at = (2 * xx + half) * part
            g_s[half, part * xx : part * (xx + 1), :] = grad_t[at : at + part]
    swap = [
        remote(g_s.at[other], pg_s, gs.at[0], gr.at[0], patch_1=other),
        remote(pa_s.at[0], pa_s.at[1], gs.at[1], gr.at[1], patch_1=other),
    ]
    for c in swap:
        c.start()
    squares = jnp.sum(error * error)
    cell = lax.broadcasted_iota(jnp.int32, (8, ROWS), 1)
    stat_s[0] = jnp.where(
        cell == 0, squares, jnp.where(cell == 1, length.astype(F32), 0.0)
    )

    def stat_copies(stage, base, n, me, to):
        return [
            remote(
                stat_s.at[stage],
                stat_s.at[base + i],
                sts.at[base + i],
                strr.at[base + i],
                **to(lax.rem(me + i, n)),
            )
            for i in range(1, n)
        ]

    stat_y = stat_copies(0, 3, 16, p, lambda t: {"patch_0": t // 2, "patch_1": lax.rem(t, 2)})
    for c in stat_y:
        c.start()
    for c in swap:
        c.wait_recv()
    left = jnp.concatenate([g_s[k], pg_s[...]], axis=1)
    right = jnp.concatenate([pa_s[0], pa_s[1]], axis=1)
    partial = dot(left, right, 1, 1)
    for xx in range(nx):
        xsend[xx] = partial[part * xx : part * (xx + 1)].astype(BF)
    xcopies = [None] * nx
    for i in range(1, nx):
        to = lax.rem(x + i, nx)
        xcopies[i] = remote(xsend.at[to], xrecv.at[i], xs.at[i], xr.at[i], dp_0=to)
        xcopies[i].start()

    for i in (1, 7, 2, 6, 3, 5, 4):
        third[i].wait_recv()

    def fold(s, carry):
        rinv = rinv_s[s // 2, 0:1, pl.ds(pl.multiple_of(lax.rem(s, 2) * ROWS, ROWS), ROWS)]
        folded = recv3[s].astype(F32) * rinv
        dof_s[s] = folded.astype(BF)
        dtok[pl.ds(pl.multiple_of(s * ROWS, ROWS), ROWS), :] = folded.T.astype(BF)
        return carry

    lax.fori_loop(0, 8, fold, 0)

    def backward(j, carry):
        grads = jnp.concatenate([dof_s[2 * j], dof_s[2 * j + 1]], axis=1)
        attn = jnp.concatenate([send2[2 * j], send2[2 * j + 1]], axis=1)
        delta = jnp.sum(grads.astype(F32) * attn.astype(F32), axis=0, keepdims=True)
        dprobs = dot(vtok[...], grads, 1, 0)
        dscores = (p_s[j].astype(F32) * (dprobs - delta)).astype(BF)
        ds_s[j] = dscores
        keys = jnp.concatenate([recv1[b, PAD : 2 * PAD, :] for b in range(16)], axis=1)
        dq = (dot(keys, dscores, 1, 0) * scale).astype(BF)
        send4[2 * j, 0:PAD, :] = dq[:, :ROWS]
        send4[2 * j + 1, 0:PAD, :] = dq[:, ROWS:]
        return carry

    lax.fori_loop(0, 4, backward, 0)

    def keyside(t, carry):
        at = pl.ds(pl.multiple_of(t * 2 * ROWS, 2 * ROWS), 2 * ROWS)
        ds_rows = jnp.concatenate([ds_s[j, at, :] for j in range(4)], axis=1)
        p_rows = jnp.concatenate([p_s[j, at, :] for j in range(4)], axis=1)
        dk = (dot(ds_rows, qtok[...], 1, 0) * scale).T.astype(BF)
        dv = dot(p_rows, dtok[...], 1, 0).T.astype(BF)
        for c in range(2):
            dkv[c, t, 0:PAD, :] = dk[:, ROWS * c : ROWS * (c + 1)]
            dkv[c, t, PAD : 2 * PAD, :] = dv[:, ROWS * c : ROWS * (c + 1)]
        return carry

    lax.fori_loop(0, 8, keyside, 0)
    cross = remote(dkv.at[other], drecv, dks.at[0], dkr.at[0], patch_1=other)
    cross.start()

    for i in range(1, nx):
        xcopies[i].wait_recv()
    total = partial[0:part] * 0.0
    total = xsend[x].astype(F32)
    for i in range(1, nx):
        total = total + xrecv[i].astype(F32)
    cols = part // zh
    for j in range(zh):
        zsend[j, 0:cols, :] = total[cols * j : cols * (j + 1)].astype(BF)
    zcopies = [None] * zh
    for j in range(zh):
        to = zh * k + j
        away = lax.rem(to - z + nz, nz)
        zcopies[j] = remote(zsend.at[j], zrecv.at[away], zs.at[j], zr.at[away], dp_1=to)

        @pl.when(to != z)
        def _():
            zcopies[j].start()

    active = z // zh == k

    @pl.when(active)
    def _():
        zrecv[0] = zsend[lax.rem(z, zh)]

    for i in range(15):
        stat_y[i].wait_recv()
    acc = stat_s[0]
    for i in range(1, 16):
        acc = acc + stat_s[3 + i]
    stat_s[1] = acc
    stat_x = stat_copies(1, 19, nx, x, lambda t: {"dp_0": t})
    for c in stat_x:
        c.start()

    cross.wait_recv()

    def join(s, carry):
        send4[s, PAD : 3 * PAD, :] = (
            dkv[k, s].astype(F32) + drecv[s].astype(F32)
        ).astype(BF)
        return carry

    lax.fori_loop(0, 8, join, 0)
    fourth = [None] * 8
    for i in FAR:
        to = lax.rem(y + i, 8)
        fourth[i] = remote(send4.at[to], recv4.at[y], s4.at[i], r4.at[i], patch_0=to)
        fourth[i].start()
    recv4[y] = send4[y]

    for c in stat_x:
        c.wait_recv()
    acc = stat_s[1]
    for i in range(1, nx):
        acc = acc + stat_s[19 + i]
    stat_s[2] = acc
    stat_z = stat_copies(2, 19 + nx, nz, z, lambda t: {"dp_1": t})
    for c in stat_z:
        c.start()

    def z_in(i):
        return remote(zsend.at[0], zrecv.at[i], zs.at[0], zr.at[i], dp_1=z)

    @pl.when(active)
    def _():
        for i in range(1, nz):
            z_in(i).wait_recv()
        summed = zrecv[0].astype(F32)
        for i in range(1, nz):
            summed = summed + zrecv[i].astype(F32)
        for t in range(16):
            ysend[t, 0:cols, 0:36] = summed[0:cols, 36 * t : 36 * (t + 1)]

    def y_out(t):
        return remote(
            ysend.at[t], yrecv.at[y], ys.at[t], yr.at[y], patch_0=t // 2, patch_1=t % 2
        )

    for t in range(16):

        @pl.when(active & (p != t))
        def _():
            y_out(t).start()

    @pl.when(active)
    def _():
        yrecv[y] = ysend[p]

    for c in stat_z:
        c.wait_recv()
    acc = stat_s[2]
    for i in range(1, nz):
        acc = acc + stat_s[19 + nx + i]
    st_out[...] = acc

    for i in (1, 7, 2, 6, 3, 5, 4):
        fourth[i].wait_recv()
    for at, out in enumerate((dq_out, dk_out, dv_out)):
        whole = jnp.concatenate(
            [
                recv4[h, PAD * at : PAD * (at + 1), :].astype(F32)[:HEAD_DIM]
                for h in range(HEADS)
            ],
            axis=0,
        )
        out[...] = whole.T

    for i in range(8):
        here = active & (y == i)

        @pl.when(jnp.logical_not(here))
        def _():
            remote(
                ysend.at[0], yrecv.at[i], ys.at[0], yr.at[i], patch_0=y, patch_1=k
            ).wait_recv()

    final = yrecv[0]
    for i in range(1, 8):
        final = final + yrecv[i]
    wg_out[...] = final

    for group in (first, second, third, fourth, xcopies):
        for c in group[1:]:
            c.wait_send()
    for c in passed + swap + [cross] + stat_y + stat_x + stat_z:
        c.wait_send()
    for j in range(zh):

        @pl.when(zh * k + j != z)
        def _():
            zcopies[j].wait_send()

    for t in range(16):

        @pl.when(active & (p != t))
        def _():
            y_out(t).wait_send()


def step(nx, nz, query_rows, key_rows, value_rows, out_weight, target, lengths, segments):
    part = WIDTH // (2 * nx)
    zh = nz // 2
    dma = pltpu.SemaphoreType.DMA
    scratch = [
        pltpu.VMEM((FEAT, WIDTH), BF),
        pltpu.VMEM((1, ROWS, WIDTH), BF),
        pltpu.VMEM((8, 3 * PAD, ROWS), BF),
        pltpu.VMEM((16, 3 * PAD, ROWS), BF),
        pltpu.VMEM((2048, PAD), BF),
        pltpu.VMEM((2048, PAD), BF),
        pltpu.VMEM((1024, PAD), BF),
        pltpu.VMEM((1024, PAD), BF),
        pltpu.VMEM((4, 2048, 256), BF),
        pltpu.VMEM((4, 2048, 256), BF),
        pltpu.VMEM((4, 8, 256), F32),
        pltpu.VMEM((8, PAD, ROWS), BF),
        pltpu.VMEM((8, PAD, ROWS), BF),
        pltpu.VMEM((FEAT, ROWS), F32),
        pltpu.VMEM((8, PAD, ROWS), BF),
        pltpu.VMEM((8, PAD, ROWS), BF),
        pltpu.VMEM((8, PAD, ROWS), BF),
        pltpu.VMEM((2, 8, 2 * PAD, ROWS), BF),
        pltpu.VMEM((8, 2 * PAD, ROWS), BF),
        pltpu.VMEM((8, 3 * PAD, ROWS), BF),
        pltpu.VMEM((8, 3 * PAD, ROWS), BF),
        pltpu.VMEM((2, FEAT, ROWS), BF),
        pltpu.VMEM((FEAT, ROWS), BF),
        pltpu.VMEM((2, FEAT, ROWS), BF),
        pltpu.VMEM((nx, part, FEAT), BF),
        pltpu.VMEM((nx, part, FEAT), BF),
        pltpu.VMEM((zh, 48, FEAT), BF),
        pltpu.VMEM((nz, 48, FEAT), BF),
        pltpu.VMEM((16, 40, 128), F32),
        pltpu.VMEM((8, 40, 128), F32),
        pltpu.VMEM((19 + nx + nz, 8, ROWS), F32),
    ]
    sems = [2, 8, 8, 8, 8, 8, 8, 8, 8, 1, 1, 8, 8, 2, 2, nx, nx, zh, nz, 16, 8]
    sems += [19 + nx + nz] * 2
    vmem = pl.BlockSpec(memory_space=pltpu.VMEM)
    hbm = pl.BlockSpec(memory_space=pl.ANY)
    wide = jax.ShapeDtypeStruct((ROWS, FEAT), F32)
    dq, dk, dv, wg, st = pl.pallas_call(
        functools.partial(body, nx, nz),
        out_shape=(
            wide,
            wide,
            wide,
            jax.ShapeDtypeStruct((40, 128), F32),
            jax.ShapeDtypeStruct((8, ROWS), F32),
        ),
        in_specs=[vmem] * 4 + [pl.BlockSpec(memory_space=pltpu.SMEM), hbm, hbm],
        out_specs=(vmem,) * 5,
        scratch_shapes=scratch + [dma((n,)) for n in sems],
        compiler_params=pltpu.CompilerParams(
            collective_id=0, has_side_effects=True, vmem_limit_bytes=60 * 1024 * 1024
        ),
    )(query_rows, key_rows, value_rows, segments, lengths, out_weight, target)
    slots = 16 * ROWS
    count = st[0, 1] / 16.0
    ratio = jnp.float32(nx * nz * slots) / count
    return (
        (ratio * dq)[None],
        (ratio * dk)[None],
        (ratio * dv)[None],
        wg[:36, :36].T * (ratio / slots),
        st[0, 0] / (count * WIDTH),
    )


def solution(mesh):
    torus = Mesh(mesh.devices.reshape(4, 8, 8, 2), ("dp_0", "dp_1", "patch_0", "patch_1"))
    return jax.shard_map(
        functools.partial(step, 4, 8),
        mesh=torus,
        in_specs=(
            P(DP, PATCH, None),
            P(DP, PATCH, None),
            P(DP, PATCH, None),
            P(),
            P(DP, PATCH, None),
            P(DP),
            P(DP, PATCH),
        ),
        out_specs=(P(DP, PATCH, None), P(DP, PATCH, None), P(DP, PATCH, None), P(PATCH, DP), P()),
        check_vma=False,
    )
```

time: 235 us -> 90.4 us (0.38)
  blocking collectives: 93.6 us -> 0 us
  Pallas kernels: 0 us -> 74 us
  waiting for transfers between devices: 51 us -> 0 us
  matrix products: 33.5 us -> 0 us
  starting transfers between devices: 19 us -> 0 us
  between operations: 18.1 us -> 4.44 us
  other arithmetic: 8.61 us -> 1.77 us
    pallas_call x0 -> x1, Pallas kernels: none -> 74 us  [step(): pl.pallas_call(functools.partial(body, nx, nz), out_shape=(wide, wide, wi...]
    psum x4 -> x0, blocking collectives: 55.2 us -> none  [by_axis(): value = lax.psum(value, axis)]
    all_gather x2 -> x0, waiting for transfers between devices: 40.1 us -> none  [sent_together(): lax.all_gather(both, axis, axis=dim, tiled=True)]
    all_gather x2 -> x0, blocking collectives: 38.4 us -> none  [the longest x1 21.1 us: local(): segment_all = lax.all_gather(segments, PATCH, axis=1, tiled=True)]
    dot_general x9 -> x0, matrix products: 33.5 us -> none  [the longest x1 9.73 us: query_grad_block(): jnp.einsum('hqk,khe->qhe', dscores, key_heads, preferred_element_type=jnp...]
    all_to_all x3 -> x0, starting transfers between devices: 18.9 us -> none  [the longest x2 10.6 us: sum_at_owner(): lax.all_to_all(in_blocks(value, dim, peers), axis, 0, 0, tiled=True)]
    all_to_all x3 -> x0, waiting for transfers between devices: 10.9 us -> none  [the longest x1 5.89 us: from_everyone(): return lax.all_to_all(copies, axis, split_axis=0, concat_axis=0, tiled=True)]
    unnamed x30 -> x11, local copies, waits for them, and re-layouts: 1.52 us -> 8.43 us
  transfers between devices with their start and end apart: 5 -> 0, of which waited for: 3 -> 0; matrix products, arithmetic and copies ran while one was open for 8% -> 0% of each run, Pallas kernels for 0% -> 0%
where the time goes in v1:
time: 90.4 us; the launch traced here: 90 us
  Pallas kernels  74 us (82%)
  local copies, waits for them, and re-layouts  9.77 us (11%)
  between operations  4.44 us (5%)
  other arithmetic  1.77 us (2%)
    pallas_call x1, Pallas kernels, step(): pl.pallas_call(functools.partial(body, nx, nz), out_shape=(wide, wide, wi...  74 us
    unnamed x11, local copies, waits for them, and re-layouts  8.43 us

profile of v1, /device:TPU:1, one launch (start us, length us, event | category | flops | bytes accessed | tf_op | source)
XLA Modules:
  0.0 90.0 jit_solution(7197641581042311494)
XLA Ops:
  1.3 1.7 %copy.12.q_ref = bf16[1,128,576]{2,1,0:T(8,128)(2,1)} copy(bf16[1,128,576]{1,2,0:T(8,128)(2,1)} %param.7) | data formatting | bytes 294912 | tf_op args[0]
  3.0 1.7 %copy.13.k_ref = bf16[1,128,576]{2,1,0:T(8,128)(2,1)} copy(bf16[1,128,576]{1,2,0:T(8,128)(2,1)} %param.8) | data formatting | bytes 294912 | tf_op args[1]
  4.7 1.7 %copy.14.v_ref = bf16[1,128,576]{2,1,0:T(8,128)(2,1)} copy(bf16[1,128,576]{1,2,0:T(8,128)(2,1)} %param.9) | data formatting | bytes 294912 | tf_op args[2]
  6.4 74.0 %shard_map.110 = (f32[128,576]{1,0:T(8,128)}, f32[128,576]{1,0:T(8,128)}, f32[128,576]{1,0:T(8,128)}, f32[40,128]{1,0:T(8,128)}, f32[8,128]{1,0:T(8,128)}) custom-call(bf16[1,128,576]{2,1,0:T(8,128)(2,1)} %copy.12.q_ref, bf16[1,128,576]{2,1,0:T(8,128)(2,1)} %copy.13.k_ref, bf16[1,128,576]{2,1,0:T(8,128)(2,1)} %copy.14.v_ref, s32[1,128]{1,0:T(1,128)} %seg_ref.1, ...), custom_call_target="tpu_custom_call" | custom-call | tf_op jit(solution)/shard_map/pallas_call | solution.py:513
  80.5 0.0 copy-start
  80.5 0.0 copy-start.1
  80.5 1.3 %fusion = (f32[1,1]{1,0:T(1,128)}, f32[1,1]{1,0:T(1,128)}) fusion(f32[8,128]{1,0:T(8,128)} %get-tuple-element.10), kind=kLoop, calls=%fused_computation.4 | loop fusion | bytes 16 | tf_op jit(solution)/shard_map/slice | solution.py:537
  83.8 0.7 multiply_bitcast_fusion.3
  84.6 0.7 copy.18
  85.2 1.0 %multiply_bitcast_fusion.2 = f32[1,128,576]{2,1,0:T(8,128)S(1)} fusion(f32[128,576]{1,0:T(8,128)} %get-tuple-element.11, f32[]{:T(128)} %bitcast), kind=kLoop, calls=%fused_computation.2 | loop fusion | flops 73728 | bytes 589828 | tf_op jit(solution)/shard_map/broadcast_in_dim | solution.py:533
  86.2 0.9 copy.15
  87.1 0.0 copy-done
  87.1 0.0 copy-done.1
  87.2 0.9 copy.17
  88.0 0.9 copy.16
  (1 shorter events, 0.0 us)
Async XLA Ops:
  80.5 6.6 %copy-start = (f32[128,576]{1,0:T(8,128)S(1)}, f32[128,576]{1,0:T(8,128)}, u32[]{:S(2)}) copy-start(f32[128,576]{1,0:T(8,128)} %get-tuple-element.12) | copy-start | bytes 884740
  80.5 6.6 %copy-start.1 = (f32[128,576]{1,0:T(8,128)S(1)}, f32[128,576]{1,0:T(8,128)}, u32[]{:S(2)}) copy-start(f32[128,576]{1,0:T(8,128)} %get-tuple-element.13) | copy-start | bytes 884740

commit v2 on v1

--- a/solution.py
+++ b/solution.py
@@ -140,7 +140,7 @@
     k_mask = MASK * (1.0 - mine)
     v_ones = jnp.where(row == 0, 1.0, 0.0).astype(F32)
     for at, (ref, extra) in enumerate(((q_ref, q_mask), (k_ref, k_mask), (v_ref, v_ones))):
-        whole = ref[0].astype(F32).T
+        whole = ref[0].astype(F32)
         for h in range(HEADS):
             block = jnp.concatenate([whole[HEAD_DIM * h : HEAD_DIM * (h + 1)], extra], axis=0)
             send1[h, PAD * at : PAD * (at + 1), :] = block.astype(BF)
@@ -422,7 +422,9 @@
     acc = stat_s[2]
     for i in range(1, nz):
         acc = acc + stat_s[19 + nx + i]
-    st_out[...] = acc
+    count = acc[0:1, 1:2] / 16.0
+    ratio = (nx * nz * 16.0 * ROWS) / count
+    st_out[...] = acc[0:1, 0:1] / (count * WIDTH)
 
     for i in (1, 7, 2, 6, 3, 5, 4):
         fourth[i].wait_recv()
@@ -434,7 +436,7 @@
             ],
             axis=0,
         )
-        out[...] = whole.T
+        out[0] = whole * ratio
 
     for i in range(8):
         here = active & (y == i)
@@ -448,7 +450,7 @@
     final = yrecv[0]
     for i in range(1, 8):
         final = final + yrecv[i]
-    wg_out[...] = final
+    wg_out[...] = final.T[0:36, 0:36] * (ratio / (16.0 * ROWS))
 
     for group in (first, second, third, fourth, xcopies):
         for c in group[1:]:
@@ -509,15 +511,15 @@
     sems += [19 + nx + nz] * 2
     vmem = pl.BlockSpec(memory_space=pltpu.VMEM)
     hbm = pl.BlockSpec(memory_space=pl.ANY)
-    wide = jax.ShapeDtypeStruct((ROWS, FEAT), F32)
+    wide = jax.ShapeDtypeStruct((1, FEAT, ROWS), F32)
     dq, dk, dv, wg, st = pl.pallas_call(
         functools.partial(body, nx, nz),
         out_shape=(
             wide,
             wide,
             wide,
-            jax.ShapeDtypeStruct((40, 128), F32),
-            jax.ShapeDtypeStruct((8, ROWS), F32),
+            jax.ShapeDtypeStruct((36, 36), F32),
+            jax.ShapeDtypeStruct((1, 1), F32),
         ),
         in_specs=[vmem] * 4 + [pl.BlockSpec(memory_space=pltpu.SMEM), hbm, hbm],
         out_specs=(vmem,) * 5,
@@ -525,16 +527,21 @@
         compiler_params=pltpu.CompilerParams(
             collective_id=0, has_side_effects=True, vmem_limit_bytes=60 * 1024 * 1024
         ),
-    )(query_rows, key_rows, value_rows, segments, lengths, out_weight, target)
-    slots = 16 * ROWS
-    count = st[0, 1] / 16.0
-    ratio = jnp.float32(nx * nz * slots) / count
+    )(
+        jnp.swapaxes(query_rows, 1, 2),
+        jnp.swapaxes(key_rows, 1, 2),
+        jnp.swapaxes(value_rows, 1, 2),
+        segments,
+        lengths,
+        out_weight,
+        target,
+    )
     return (
-        (ratio * dq)[None],
-        (ratio * dk)[None],
-        (ratio * dv)[None],
-        wg[:36, :36].T * (ratio / slots),
-        st[0, 0] / (count * WIDTH),
+        jnp.swapaxes(dq, 1, 2),
+        jnp.swapaxes(dk, 1, 2),
+        jnp.swapaxes(dv, 1, 2),
+        wg,
+        st[0, 0],
     )
 
 

time: 90.4 us -> 82 us (0.907)
  local copies, waits for them, and re-layouts: 9.77 us -> 4.76 us
  other arithmetic: 1.77 us -> 0 us
  between operations: 4.44 us -> 3.07 us
    unnamed x11 -> x8, local copies, waits for them, and re-layouts: 8.43 us -> 4.76 us
    slice x1 -> x0, local copies, waits for them, and re-layouts: 1.34 us -> none  [step(): st[0, 0] / (count * WIDTH)]
    broadcast_in_dim x2 -> x0, other arithmetic: 1.04 us -> none  [the longest x1 1 us: step(): (ratio * dq)[None]]
where the time goes in v2:
time: 82 us; the launch traced here: 81.7 us
  Pallas kernels  73.9 us (90%)
  local copies, waits for them, and re-layouts  4.76 us (6%)
  between operations  3.07 us (4%)
    pallas_call x1, Pallas kernels, step(): pl.pallas_call(functools.partial(body, nx, nz), out_shape=(wide, wide, wi...  73.9 us
    unnamed x8, local copies, waits for them, and re-layouts  4.76 us

profile of v2, /device:TPU:1, one launch (start us, length us, event | category | flops | bytes accessed | tf_op | source)
XLA Modules:
  0.0 81.7 jit_solution(9641366027363733005)
XLA Ops:
  1.3 73.9 %shard_map.110 = (f32[1,576,128]{2,1,0:T(8,128)}, f32[1,576,128]{2,1,0:T(8,128)}, f32[1,576,128]{2,1,0:T(8,128)}, f32[36,36]{1,0:T(8,128)}, f32[1,1]{1,0:T(1,128)}) custom-call(bf16[1,576,128]{2,1,0:T(8,128)(2,1)} %bitcast.10, bf16[1,576,128]{2,1,0:T(8,128)(2,1)} %bitcast.11, bf16[1,576,128]{2,1,0:T(8,128)(2,1)} %bitcast.12, s32[1,128]{1,0:T(1,128)} %seg_ref.1, ...), custom_call_target="tpu_custom_call" | custom-call | tf_op jit(solution)/shard_map/pallas_call | solution.py:515
  75.2 0.0 copy-start
  75.2 0.0 copy-start.1
  75.2 1.7 %copy.18 = f32[1,128,576]{1,2,0:T(8,128)} copy(f32[1,128,576]{1,2,0:T(8,128)} %bitcast.9) | data formatting | bytes 589824
  77.0 1.7 %copy.19 = f32[1,128,576]{1,2,0:T(8,128)} copy(f32[1,128,576]{1,2,0:T(8,128)} %bitcast.8) | data formatting | bytes 589824
  78.7 0.0 copy-done
  78.7 0.7 copy.20
  79.4 0.0 copy-done.1
  79.4 0.6 copy.21
Async XLA Ops:
  75.2 3.5 %copy-start = (f32[1,576,128]{2,1,0:T(8,128)S(1)}, f32[1,576,128]{2,1,0:T(8,128)}, u32[]{:S(2)}) copy-start(f32[1,576,128]{2,1,0:T(8,128)} %get-tuple-element.12) | copy-start | bytes 884740
  75.2 4.2 %copy-start.1 = (f32[36,36]{1,0:T(8,128)S(1)}, f32[36,36]{1,0:T(8,128)}, u32[]{:S(2)}) copy-start(f32[36,36]{1,0:T(8,128)} %get-tuple-element.23) | copy-start | bytes 15556

commit v3 on v2

v3 whole, which is shorter than its diff:
```python
import functools
import math

import jax
import jax.numpy as jnp
from jax import lax
from jax.experimental import pallas as pl
from jax.experimental.pallas import tpu as pltpu
from jax.sharding import Mesh
from jax.sharding import PartitionSpec as P

WIDTH = 1152
HEADS = 8
HEAD_DIM = 72
FEAT = 576
ROWS = 128
PAD = 80
PATCH = ("patch_0", "patch_1")
DP = ("dp_0", "dp_1")
BF = jnp.bfloat16
F32 = jnp.float32
FAR = (4, 3, 5, 2, 6, 1, 7)
NEAR = (1, 7, 2, 6, 3, 5, 4)
LAG = 3
MASK = 2.0**50


def dot(a, b, ca, cb):
    return lax.dot_general(a, b, (((ca,), (cb,)), ((), ())), preferred_element_type=F32)


def body(
    nx,
    nz,
    q_hbm,
    k_hbm,
    v_hbm,
    seg_hbm,
    len_ref,
    w_hbm,
    t_hbm,
    dq_out,
    dk_out,
    dv_out,
    wg_out,
    st_out,
    q_s,
    k_s,
    v_s,
    seg_s,
    w_s,
    t_s,
    send1,
    recv1,
    ktok,
    vtok,
    qtok,
    dtok,
    p_s,
    ds_s,
    rinv_s,
    send2,
    recv2,
    at_s,
    send3,
    recv3,
    dkv,
    drecv,
    send4,
    recv4,
    g_s,
    pg_s,
    pa_s,
    xsend,
    xrecv,
    zsend,
    zrecv,
    ysend,
    yrecv,
    stat_s,
    load_sem,
    s1,
    r1,
    s1v,
    r1v,
    d1s,
    d1r,
    d1vs,
    d1vr,
    s2,
    r2,
    s3,
    r3,
    dks,
    dkr,
    s4q,
    r4q,
    s4,
    r4,
    gs,
    gr,
    xs,
    xr,
    zs,
    zr,
    ys,
    yr,
    sts,
    strr,
):
    x = lax.axis_index("dp_0")
    z = lax.axis_index("dp_1")
    y = lax.axis_index("patch_0")
    k = lax.axis_index("patch_1")
    other = 1 - k
    p = 2 * y + k
    zh = nz // 2
    scale = 1.0 / math.sqrt(HEAD_DIM)

    loads = [
        pltpu.make_async_copy(src, dst, load_sem.at[n])
        for n, (src, dst) in enumerate(
            (
                (q_hbm, q_s),
                (k_hbm, k_s),
                (seg_hbm, seg_s),
                (v_hbm, v_s),
                (w_hbm, w_s),
                (t_hbm, t_s),
            )
        )
    ]
    for c in loads:
        c.start()

    barrier = pltpu.get_barrier_semaphore()
    for i in range(1, 8):
        peer = lax.rem(y + i, 8)
        pl.semaphore_signal(barrier, inc=1, device_id={"patch_0": peer})
        pl.semaphore_signal(barrier, inc=1, device_id={"patch_0": peer, "patch_1": other})
    pl.semaphore_signal(barrier, inc=1, device_id={"patch_1": other})
    for i in range(1, nx):
        pl.semaphore_signal(barrier, inc=1, device_id={"dp_0": lax.rem(x + i, nx)})
    for i in range(1, nz):
        pl.semaphore_signal(barrier, inc=1, device_id={"dp_1": lax.rem(z + i, nz)})

    def remote(src, dst, ssem, rsem, **where):
        return pltpu.make_async_remote_copy(
            src_ref=src, dst_ref=dst, send_sem=ssem, recv_sem=rsem, device_id=where
        )

    row = lax.broadcasted_iota(jnp.int32, (8, ROWS), 0)
    lane = lax.broadcasted_iota(jnp.int32, (8, ROWS), 1)
    length = len_ref[0]
    live_t = p * ROWS + lane < length
    for c in loads[:4]:
        c.wait()
    code = jnp.where(live_t, jnp.broadcast_to(seg_s[...], (8, ROWS)), 8)
    low = jnp.bitwise_and(row, 3)
    weight = jnp.where(low == 0, 1, jnp.where(low == 1, 2, jnp.where(low == 2, 4, 8)))
    bit = jnp.where(jnp.bitwise_and(code, weight) != 0, 1.0, 0.0).astype(F32)
    mine = jnp.where(row < 4, bit, 1.0 - bit)
    q_mask = -MASK * mine
    k_mask = MASK * (1.0 - mine)
    v_ones = jnp.where(row == 0, 1.0, 0.0).astype(F32)
    for at, (ref, extra) in enumerate(((q_s, q_mask), (k_s, k_mask), (v_s, v_ones))):
        whole = ref[0].astype(F32)
        for h in range(HEADS):
            block = jnp.concatenate([whole[HEAD_DIM * h : HEAD_DIM * (h + 1)], extra], axis=0)
            send1[h, PAD * at : PAD * (at + 1), :] = block.astype(BF)
    recv1[p] = send1[y]

    pl.semaphore_wait(barrier, 15 + (nx - 1) + (nz - 1))

    qk = pl.ds(0, 2 * PAD)
    ko = pl.ds(PAD, PAD)
    vo = pl.ds(2 * PAD, PAD)

    def spread(rows, ssem, rsem):
        out = [None] * 8
        for i in FAR:
            h = lax.rem(y + i, 8)
            out[i] = remote(
                send1.at[h, rows], recv1.at[p, rows], ssem.at[i], rsem.at[i], patch_0=h
            )
            out[i].start()
        return out

    first = spread(qk, s1, r1)
    first_v = spread(vo, s1v, r1v)

    def source(i):
        return lax.rem(y - i + 8, 8)

    def pass_on(i, rows, ssem, rsem):
        ref = recv1.at[2 * source(i) + k, rows]
        return remote(ref, ref, ssem.at[i], rsem.at[i], patch_1=other)

    def token_major(dst, b, part, at):
        at = pl.ds(pl.multiple_of(at * ROWS, ROWS), ROWS)
        dst[at, :] = recv1[b, PAD * part : PAD * (part + 1), :].astype(F32).T.astype(BF)

    passed = [pass_on(i, ko, d1s, d1r) for i in range(8)]
    passed_v = [pass_on(i, vo, d1vs, d1vr) for i in range(8)]
    passed[0].start()
    passed_v[0].start()
    token_major(ktok, p, 1, p)
    for i in NEAR:
        first[i].wait_recv()
        passed[i].start()
        b = 2 * source(i) + k
        token_major(ktok, b, 1, b)
    for i in (0,) + NEAR:
        passed[i].wait_recv()
        b = 2 * source(i) + other
        token_major(ktok, b, 1, b)

    factor = scale * math.log2(math.e)
    pair = y // 2
    mate = y + 1 - 2 * lax.rem(y, 2)

    def forward(j, carry):
        queries = jnp.concatenate([recv1[4 * j + k, 0:PAD, :], recv1[4 * j + 2 + k, 0:PAD, :]], axis=1)
        scores = dot(ktok[...], queries, 1, 0)
        top = jnp.max(scores, axis=0, keepdims=True)
        p_s[j] = jnp.exp2((scores - top) * factor).astype(BF)
        return carry

    lax.fori_loop(0, 4, forward, 0)
    for i in NEAR:
        first_v[i].wait_recv()
        passed_v[i].start()
    for i in (0,) + NEAR:
        passed_v[i].wait_recv()

    def send_attn(s):
        i = lax.rem(s - y + 8, 8)
        return remote(send2.at[s], recv2.at[y], s2.at[i], r2.at[i], patch_0=s)

    for step_at in (2, 1, 3, 0):
        j = lax.rem(pair + step_at, 4)
        values = jnp.concatenate([recv1[b, 2 * PAD : 3 * PAD, :] for b in range(16)], axis=1)
        accum = dot(values, p_s[j], 1, 0)
        rinv = 1.0 / accum[HEAD_DIM : HEAD_DIM + 1, :]
        rinv_s[j] = jnp.broadcast_to(rinv, (8, 2 * ROWS))
        attn = (accum * rinv).astype(BF)
        send2[2 * j] = attn[:, :ROWS]
        send2[2 * j + 1] = attn[:, ROWS:]
        if step_at:
            send_attn(2 * j).start()
            send_attn(2 * j + 1).start()
        else:
            send_attn(mate).start()
    recv2[y] = send2[y]

    def backward_layouts(b, carry):
        token_major(vtok, b, 2, b)
        return carry

    lax.fori_loop(0, 16, backward_layouts, 0)

    def query_layouts(src, carry):
        token_major(qtok, 2 * src + k, 0, src)
        return carry

    lax.fori_loop(0, 8, query_layouts, 0)

    loads[4].wait()
    loads[5].wait()
    for i in NEAR:
        remote(send2.at[y], recv2.at[source(i)], s2.at[i], r2.at[i], patch_0=source(i)).wait_recv()
    for h in range(HEADS):
        at_s[HEAD_DIM * h : HEAD_DIM * (h + 1), :] = recv2[h].astype(F32)[:HEAD_DIM]
    attn_t = at_s[...].astype(BF)
    pa_s[0] = attn_t
    swap_a = remote(pa_s.at[0], pa_s.at[1], gs.at[1], gr.at[1], patch_1=other)
    swap_a.start()
    output = dot(attn_t, w_s[...], 0, 0)
    token = lax.broadcasted_iota(jnp.int32, (ROWS, WIDTH), 0)
    live = p * ROWS + token < length
    error = jnp.where(live, output - t_s[0].astype(F32), 0.0)
    grad_out = (2.0 * error).astype(BF)
    grad_attn = dot(w_s[...], grad_out, 1, 1)
    for h in range(HEADS):
        block = jnp.concatenate(
            [grad_attn[HEAD_DIM * h : HEAD_DIM * (h + 1)], jnp.zeros((8, ROWS), F32)], axis=0
        )
        send3[h] = block.astype(BF)
    third = [None] * 8
    for i in FAR:
        to = lax.rem(y + i, 8)
        third[i] = remote(send3.at[to], recv3.at[y], s3.at[i], r3.at[i], patch_0=to)
        third[i].start()
    recv3[y] = send3[y]

    grad_t = (2.0 * error).T.astype(BF)
    part = WIDTH // (2 * nx)
    for half in range(2):
        for xx in range(nx):
            at = (2 * xx + half) * part
            g_s[half, part * xx : part * (xx + 1), :] = grad_t[at : at + part]
    swap_g = remote(g_s.at[other], pg_s, gs.at[0], gr.at[0], patch_1=other)
    swap_g.start()
    squares = jnp.sum(error * error)
    cell = lax.broadcasted_iota(jnp.int32, (8, ROWS), 1)
    stat_s[0] = jnp.where(
        cell == 0, squares, jnp.where(cell == 1, length.astype(F32), 0.0)
    )

    def stat_copies(stage, base, n, me, to):
        return [
            remote(
                stat_s.at[stage],
                stat_s.at[base + i],
                sts.at[base + i],
                strr.at[base + i],
                **to(lax.rem(me + i, n)),
            )
            for i in range(1, n)
        ]

    def stat_sum(stage, base, n, copies):
        for c in copies:
            c.wait_recv()
        acc = stat_s[stage]
        for i in range(1, n):
            acc = acc + stat_s[base + i]
        return acc

    stat_y = stat_copies(0, 3, 16, p, lambda t: {"patch_0": t // 2, "patch_1": lax.rem(t, 2)})
    for c in stat_y:
        c.start()
    swap_a.wait_recv()
    swap_g.wait_recv()
    left = jnp.concatenate([g_s[k], pg_s[...]], axis=1)
    right = jnp.concatenate([pa_s[0], pa_s[1]], axis=1)
    partial = dot(left, right, 1, 1)
    for xx in range(nx):
        xsend[xx] = partial[part * xx : part * (xx + 1)].astype(BF)
    xcopies = [None] * nx
    for i in range(1, nx):
        to = lax.rem(x + i, nx)
        xcopies[i] = remote(xsend.at[to], xrecv.at[i], xs.at[i], xr.at[i], dp_0=to)
        xcopies[i].start()

    def send_grad(s, rows, ssem, rsem):
        i = lax.rem(s - y + 8, 8)
        return remote(
            send4.at[s, rows], recv4.at[y, rows], ssem.at[i], rsem.at[i], patch_0=s
        )

    qo = pl.ds(0, PAD)
    kvo = pl.ds(PAD, 2 * PAD)

    def third_in(s):
        i = lax.rem(y - s + 8, 8)
        remote(send3.at[y], recv3.at[s], s3.at[i], r3.at[i], patch_0=s).wait_recv()

    for step_at in (0, 1, 3, 2):
        j = lax.rem(pair + step_at, 4)
        if step_at:
            third_in(2 * j)
            third_in(2 * j + 1)
        else:
            third_in(mate)
        grads = jnp.concatenate([recv3[2 * j], recv3[2 * j + 1]], axis=1).astype(F32)
        folded = grads * rinv_s[j, 0:1, :]
        dtok[pl.ds(pl.multiple_of(j * 2 * ROWS, 2 * ROWS), 2 * ROWS), :] = folded.T.astype(BF)
        folded = folded.astype(BF)
        attn = jnp.concatenate([send2[2 * j], send2[2 * j + 1]], axis=1)
        delta = jnp.sum(folded.astype(F32) * attn.astype(F32), axis=0, keepdims=True)
        dprobs = dot(vtok[...], folded, 1, 0)
        dscores = (p_s[j].astype(F32) * (dprobs - delta)).astype(BF)
        ds_s[j] = dscores
        keys = jnp.concatenate([recv1[b, PAD : 2 * PAD, :] for b in range(16)], axis=1)
        dq = (dot(keys, dscores, 1, 0) * scale).astype(BF)
        send4[2 * j, 0:PAD, :] = dq[:, :ROWS]
        send4[2 * j + 1, 0:PAD, :] = dq[:, ROWS:]
        if step_at:
            send_grad(2 * j, qo, s4q, r4q).start()
            send_grad(2 * j + 1, qo, s4q, r4q).start()
        else:
            send_grad(mate, qo, s4q, r4q).start()

    stat_s[1] = stat_sum(0, 3, 16, stat_y)
    stat_x = stat_copies(1, 19, nx, x, lambda t: {"dp_0": t})
    for c in stat_x:
        c.start()

    def crossing(t):
        i = lax.rem(t - y + 8, 8)
        return remote(dkv.at[other, t], drecv.at[t], dks.at[i], dkr.at[i], patch_1=other)

    def join(t, away):
        crossing(t).wait_recv()
        send4[t, PAD : 3 * PAD, :] = (
            dkv[k, t].astype(F32) + drecv[t].astype(F32)
        ).astype(BF)
        if away:
            send_grad(t, kvo, s4, r4).start()

    order = FAR + (0,)
    for n, i in enumerate(order):
        t = lax.rem(y + i, 8)
        at = pl.ds(pl.multiple_of(t * 2 * ROWS, 2 * ROWS), 2 * ROWS)
        ds_rows = jnp.concatenate([ds_s[j, at, :] for j in range(4)], axis=1)
        p_rows = jnp.concatenate([p_s[j, at, :] for j in range(4)], axis=1)
        dk = (dot(ds_rows, qtok[...], 1, 0) * scale).T.astype(BF)
        dv = dot(p_rows, dtok[...], 1, 0).T.astype(BF)
        for c in range(2):
            dkv[c, t, 0:PAD, :] = dk[:, ROWS * c : ROWS * (c + 1)]
            dkv[c, t, PAD : 2 * PAD, :] = dv[:, ROWS * c : ROWS * (c + 1)]
        crossing(t).start()
        if n >= LAG:
            join(lax.rem(y + order[n - LAG], 8), order[n - LAG])
    for i in order[8 - LAG :]:
        join(lax.rem(y + i, 8), i)

    for i in range(1, nx):
        xcopies[i].wait_recv()
    total = xsend[x].astype(F32)
    for i in range(1, nx):
        total = total + xrecv[i].astype(F32)
    cols = part // zh
    for j in range(zh):
        zsend[j, 0:cols, :] = total[cols * j : cols * (j + 1)].astype(BF)
    zcopies = [None] * zh
    for j in range(zh):
        to = zh * k + j
        away = lax.rem(to - z + nz, nz)
        zcopies[j] = remote(zsend.at[j], zrecv.at[away], zs.at[j], zr.at[away], dp_1=to)

        @pl.when(to != z)
        def _():
            zcopies[j].start()

    active = z // zh == k

    @pl.when(active)
    def _():
        zrecv[0] = zsend[lax.rem(z, zh)]

    stat_s[2] = stat_sum(1, 19, nx, stat_x)
    stat_z = stat_copies(2, 19 + nx, nz, z, lambda t: {"dp_1": t})
    for c in stat_z:
        c.start()
    recv4[y] = send4[y]

    def z_in(i):
        return remote(zsend.at[0], zrecv.at[i], zs.at[0], zr.at[i], dp_1=z)

    @pl.when(active)
    def _():
        for i in range(1, nz):
            z_in(i).wait_recv()
        summed = zrecv[0].astype(F32)
        for i in range(1, nz):
            summed = summed + zrecv[i].astype(F32)
        for t in range(16):
            ysend[t, 0:cols, 0:36] = summed[0:cols, 36 * t : 36 * (t + 1)]

    def y_out(t):
        return remote(
            ysend.at[t], yrecv.at[y], ys.at[t], yr.at[y], patch_0=t // 2, patch_1=t % 2
        )

    for t in range(16):

        @pl.when(active & (p != t))
        def _():
            y_out(t).start()

    @pl.when(active)
    def _():
        yrecv[y] = ysend[p]

    acc = stat_sum(2, 19 + nx, nz, stat_z)
    count = acc[0:1, 1:2] / 16.0
    ratio = (nx * nz * 16.0 * ROWS) / count
    st_out[...] = acc[0:1, 0:1] / (count * WIDTH)

    def grad_in(i, rows, ssem, rsem):
        remote(
            send4.at[y, rows], recv4.at[source(i), rows], ssem.at[i], rsem.at[i], patch_0=y
        ).wait_recv()

    def emit(at, out):
        whole = jnp.concatenate(
            [
                recv4[h, PAD * at : PAD * (at + 1), :].astype(F32)[:HEAD_DIM]
                for h in range(HEADS)
            ],
            axis=0,
        )
        out[0] = whole * ratio

    for i in NEAR:
        grad_in(i, qo, s4q, r4q)
    emit(0, dq_out)
    for i in NEAR:
        grad_in(i, kvo, s4, r4)
    emit(1, dk_out)
    emit(2, dv_out)

    for i in range(8):
        here = active & (y == i)

        @pl.when(jnp.logical_not(here))
        def _():
            remote(
                ysend.at[0], yrecv.at[i], ys.at[0], yr.at[i], patch_0=y, patch_1=k
            ).wait_recv()

    final = yrecv[0]
    for i in range(1, 8):
        final = final + yrecv[i]
    wg_out[...] = final.T[0:36, 0:36] * (ratio / (16.0 * ROWS))

    for group in (first, first_v, third, xcopies):
        for c in group[1:]:
            c.wait_send()
    for i in range(1, 8):
        to = lax.rem(y + i, 8)
        send_attn(to).wait_send()
        send_grad(to, qo, s4q, r4q).wait_send()
        send_grad(to, kvo, s4, r4).wait_send()
    for i in range(8):
        crossing(lax.rem(y + i, 8)).wait_send()
    for c in passed + passed_v + [swap_a, swap_g] + stat_y + stat_x + stat_z:
        c.wait_send()
    for j in range(zh):

        @pl.when(zh * k + j != z)
        def _():
            zcopies[j].wait_send()

    for t in range(16):

        @pl.when(active & (p != t))
        def _():
            y_out(t).wait_send()


def write_out(*refs):
    n = len(refs) // 2
    copies = [
        pltpu.make_async_copy(refs[i], refs[n + i], refs[-1].at[i]) for i in range(n)
    ]
    for c in copies:
        c.start()
    for c in copies:
        c.wait()


def step(nx, nz, query_rows, key_rows, value_rows, out_weight, target, lengths, segments):
    part = WIDTH // (2 * nx)
    zh = nz // 2
    dma = pltpu.SemaphoreType.DMA
    scratch = [
        pltpu.VMEM((1, FEAT, ROWS), BF),
        pltpu.VMEM((1, FEAT, ROWS), BF),
        pltpu.VMEM((1, FEAT, ROWS), BF),
        pltpu.VMEM((1, ROWS), jnp.int32),
        pltpu.VMEM((FEAT, WIDTH), BF),
        pltpu.VMEM((1, ROWS, WIDTH), BF),
        pltpu.VMEM((8, 3 * PAD, ROWS), BF),
        pltpu.VMEM((16, 3 * PAD, ROWS), BF),
        pltpu.VMEM((2048, PAD), BF),
        pltpu.VMEM((2048, PAD), BF),
        pltpu.VMEM((1024, PAD), BF),
        pltpu.VMEM((1024, PAD), BF),
        pltpu.VMEM((4, 2048, 256), BF),
        pltpu.VMEM((4, 2048, 256), BF),
        pltpu.VMEM((4, 8, 256), F32),
        pltpu.VMEM((8, PAD, ROWS), BF),
        pltpu.VMEM((8, PAD, ROWS), BF),
        pltpu.VMEM((FEAT, ROWS), F32),
        pltpu.VMEM((8, PAD, ROWS), BF),
        pltpu.VMEM((8, PAD, ROWS), BF),
        pltpu.VMEM((2, 8, 2 * PAD, ROWS), BF),
        pltpu.VMEM((8, 2 * PAD, ROWS), BF),
        pltpu.VMEM((8, 3 * PAD, ROWS), BF),
        pltpu.VMEM((8, 3 * PAD, ROWS), BF),
        pltpu.VMEM((2, FEAT, ROWS), BF),
        pltpu.VMEM((FEAT, ROWS), BF),
        pltpu.VMEM((2, FEAT, ROWS), BF),
        pltpu.VMEM((nx, part, FEAT), BF),
        pltpu.VMEM((nx, part, FEAT), BF),
        pltpu.VMEM((zh, 48, FEAT), BF),
        pltpu.VMEM((nz, 48, FEAT), BF),
        pltpu.VMEM((16, 40, 128), F32),
        pltpu.VMEM((8, 40, 128), F32),
        pltpu.VMEM((19 + nx + nz, 8, ROWS), F32),
    ]
    sems = [6] + [8] * 18 + [2, 2, nx, nx, zh, nz, 16, 8]
    sems += [19 + nx + nz] * 2
    vmem = pl.BlockSpec(memory_space=pltpu.VMEM)
    hbm = pl.BlockSpec(memory_space=pltpu.HBM)
    wide = jax.ShapeDtypeStruct((1, FEAT, ROWS), F32)
    results = (
        wide,
        wide,
        wide,
        jax.ShapeDtypeStruct((36, 36), F32),
        jax.ShapeDtypeStruct((1, 1), F32),
    )
    far = lambda a: pltpu.with_memory_space_constraint(a, pltpu.HBM)
    grads = pl.pallas_call(
        functools.partial(body, nx, nz),
        out_shape=results,
        in_specs=[hbm] * 4 + [pl.BlockSpec(memory_space=pltpu.SMEM), hbm, hbm],
        out_specs=(vmem,) * 5,
        scratch_shapes=scratch + [dma((n,)) for n in sems],
        compiler_params=pltpu.CompilerParams(
            collective_id=0, has_side_effects=True, vmem_limit_bytes=40 * 1024 * 1024
        ),
    )(
        far(jnp.swapaxes(query_rows, 1, 2)),
        far(jnp.swapaxes(key_rows, 1, 2)),
        far(jnp.swapaxes(value_rows, 1, 2)),
        far(segments),
        lengths,
        far(out_weight),
        far(target),
    )
    dq, dk, dv, wg, st = pl.pallas_call(
        write_out,
        out_shape=results,
        in_specs=[pl.BlockSpec(memory_space=pl.ANY)] * 5,
        out_specs=(hbm,) * 5,
        scratch_shapes=[dma((5,))],
        compiler_params=pltpu.CompilerParams(vmem_limit_bytes=2 * 1024 * 1024),
    )(*grads)
    return (
        jnp.swapaxes(dq, 1, 2),
        jnp.swapaxes(dk, 1, 2),
        jnp.swapaxes(dv, 1, 2),
        wg,
        st[0, 0],
    )


def solution(mesh):
    torus = Mesh(mesh.devices.reshape(4, 8, 8, 2), ("dp_0", "dp_1", "patch_0", "patch_1"))
    return jax.shard_map(
        functools.partial(step, 4, 8),
        mesh=torus,
        in_specs=(
            P(DP, PATCH, None),
            P(DP, PATCH, None),
            P(DP, PATCH, None),
            P(),
            P(DP, PATCH, None),
            P(DP),
            P(DP, PATCH),
        ),
        out_specs=(P(DP, PATCH, None), P(DP, PATCH, None), P(DP, PATCH, None), P(PATCH, DP), P()),
        check_vma=False,
    )
```

time: 82 us -> 71.6 us (0.87)
  local copies, waits for them, and re-layouts: 4.76 us -> 0 us
  Pallas kernels: 73.9 us -> 69.3 us
  between operations: 3.07 us -> 1.29 us
    unnamed x8 -> x0, local copies, waits for them, and re-layouts: 4.76 us -> none
    pallas_call x1 -> x2, Pallas kernels: 73.9 us -> 69.3 us  [the longest x1 67.8 us: step(): pl.pallas_call(functools.partial(body, nx, nz), out_shape=results, in_spe...]
where the time goes in v3:
time: 71.6 us; the launch traced here: 70.6 us
  Pallas kernels  69.3 us (97%)
  between operations  1.29 us (2%)
    pallas_call x1, Pallas kernels, step(): pl.pallas_call(functools.partial(body, nx, nz), out_shape=results, in_spe...  67.8 us
    pallas_call x1, Pallas kernels, step(): pl.pallas_call(write_out, out_shape=results, in_specs=[pl.BlockSpec(memor...  1.59 us

profile of v3, /device:TPU:1, one launch (start us, length us, event | category | flops | bytes accessed | tf_op | source)
XLA Modules:
  0.0 70.6 jit_solution(9164941939813604639)
XLA Ops:
  1.3 67.8 %shard_map.110 = (f32[1,576,128]{2,1,0:T(8,128)S(1)}, f32[1,576,128]{2,1,0:T(8,128)S(1)}, f32[1,576,128]{2,1,0:T(8,128)S(1)}, f32[36,36]{1,0:T(8,128)S(1)}, f32[1,1]{1,0:T(1,128)}) custom-call(bf16[1,576,128]{2,1,0:T(8,128)(2,1)} %bitcast.7, bf16[1,576,128]{2,1,0:T(8,128)(2,1)} %bitcast.8, bf16[1,576,128]{2,1,0:T(8,128)(2,1)} %bitcast.9, s32[1,128]{1,0:T(1,128)} %seg_hbm.1, ...), custom_call_target="tpu_custom_call" | custom-call | tf_op jit(solution)/shard_map/pallas_call | solution.py:608
  69.0 1.6 %shard_map.111 = (f32[1,576,128]{2,1,0:T(8,128)}, f32[1,576,128]{2,1,0:T(8,128)}, f32[1,576,128]{2,1,0:T(8,128)}, f32[36,36]{1,0:T(8,128)}, f32[1,1]{1,0:T(1,128)}) custom-call(f32[1,576,128]{2,1,0:T(8,128)S(1)} %get-tuple-element.15.refs_0_, f32[1,576,128]{2,1,0:T(8,128)S(1)} %get-tuple-element.16.refs_1_, f32[1,576,128]{2,1,0:T(8,128)S(1)} %get-tuple-element.17.refs_2_, ...), custom_call_target="tpu_custom_call" | custom-call | tf_op jit(solution)/shard_map/pallas_call | solution.py:626

commit v4 on v3

--- a/solution.py
+++ b/solution.py
@@ -22,6 +22,8 @@
 FAR = (4, 3, 5, 2, 6, 1, 7)
 NEAR = (1, 7, 2, 6, 3, 5, 4)
 LAG = 3
+XAT = 3
+ZROWS = 48
 MASK = 2.0**50
 
 
@@ -72,41 +74,28 @@
     pg_s,
     pa_s,
     xsend,
-    xrecv,
+    xrel,
+    xacc,
+    xin,
     zsend,
     zrecv,
     ysend,
     yrecv,
     stat_s,
+    relay,
     load_sem,
-    s1,
+    snd,
+    rcv,
     r1,
-    s1v,
     r1v,
-    d1s,
+    rls,
+    rlr,
     d1r,
-    d1vs,
     d1vr,
-    s2,
-    r2,
-    s3,
     r3,
-    dks,
     dkr,
-    s4q,
-    r4q,
-    s4,
-    r4,
-    gs,
-    gr,
     xs,
     xr,
-    zs,
-    zr,
-    ys,
-    yr,
-    sts,
-    strr,
 ):
     x = lax.axis_index("dp_0")
     z = lax.axis_index("dp_1")
@@ -176,40 +165,69 @@
     ko = pl.ds(PAD, PAD)
     vo = pl.ds(2 * PAD, PAD)
 
-    def spread(rows, ssem, rsem):
-        out = [None] * 8
+    two_on = lax.rem(y + 2, 8)
+
+    def spread(rows, n, rsem):
         for i in FAR:
             h = lax.rem(y + i, 8)
-            out[i] = remote(
-                send1.at[h, rows], recv1.at[p, rows], ssem.at[i], rsem.at[i], patch_0=h
+            direct = remote(
+                send1.at[h, rows], recv1.at[p, rows], snd.at[n], rsem.at[i], patch_0=h
             )
-            out[i].start()
-        return out
-
-    first = spread(qk, s1, r1)
-    first_v = spread(vo, s1v, r1v)
+            if i != 4:
+                direct.start()
+                continue
+
+            @pl.when(k == 0)
+            def _():
+                direct.start()
+
+            @pl.when(k == 1)
+            def _():
+                remote(
+                    send1.at[h, rows], relay.at[rows], snd.at[n], rlr.at[n], patch_0=two_on
+                ).start()
+
+    def relay_on(rows, n, rsem):
+        at = recv1.at[2 * lax.rem(y + 6, 8) + k, rows]
+        return remote(relay.at[rows], at, rls.at[n], rsem.at[4], patch_0=two_on)
+
+    def relay_in(rows, n, rsem):
+        @pl.when(k == 1)
+        def _():
+            remote(relay.at[rows], relay.at[rows], rls.at[n], rlr.at[n], patch_0=y).wait_recv()
+            relay_on(rows, n, rsem).start()
+
+    def block_in(i, rows, rsem):
+        b = recv1.at[2 * source(i) + k, rows]
+        remote(b, b, snd.at[0], rsem.at[i], patch_0=y).wait_recv()
+
+    spread(qk, 0, r1)
+    spread(vo, 1, r1v)
 
     def source(i):
         return lax.rem(y - i + 8, 8)
 
-    def pass_on(i, rows, ssem, rsem):
+    def pass_on(i, rows, n, rsem):
         ref = recv1.at[2 * source(i) + k, rows]
-        return remote(ref, ref, ssem.at[i], rsem.at[i], patch_1=other)
+        return remote(ref, ref, snd.at[n], rsem.at[i], patch_1=other)
 
     def token_major(dst, b, part, at):
         at = pl.ds(pl.multiple_of(at * ROWS, ROWS), ROWS)
         dst[at, :] = recv1[b, PAD * part : PAD * (part + 1), :].astype(F32).T.astype(BF)
 
-    passed = [pass_on(i, ko, d1s, d1r) for i in range(8)]
-    passed_v = [pass_on(i, vo, d1vs, d1vr) for i in range(8)]
+    passed = [pass_on(i, ko, 2, d1r) for i in range(8)]
+    passed_v = [pass_on(i, vo, 3, d1vr) for i in range(8)]
     passed[0].start()
     passed_v[0].start()
     token_major(ktok, p, 1, p)
     for i in NEAR:
-        first[i].wait_recv()
+        if i == 2:
+            relay_in(qk, 0, r1)
+        block_in(i, qk, r1)
         passed[i].start()
         b = 2 * source(i) + k
         token_major(ktok, b, 1, b)
+    relay_in(vo, 1, r1v)
     for i in (0,) + NEAR:
         passed[i].wait_recv()
         b = 2 * source(i) + other
@@ -228,14 +246,13 @@
 
     lax.fori_loop(0, 4, forward, 0)
     for i in NEAR:
-        first_v[i].wait_recv()
+        block_in(i, vo, r1v)
         passed_v[i].start()
     for i in (0,) + NEAR:
         passed_v[i].wait_recv()
 
     def send_attn(s):
-        i = lax.rem(s - y + 8, 8)
-        return remote(send2.at[s], recv2.at[y], s2.at[i], r2.at[i], patch_0=s)
+        return remote(send2.at[s], recv2.at[y], snd.at[4], rcv.at[0], patch_0=s)
 
     for step_at in (2, 1, 3, 0):
         j = lax.rem(pair + step_at, 4)
@@ -267,13 +284,13 @@
 
     loads[4].wait()
     loads[5].wait()
-    for i in NEAR:
-        remote(send2.at[y], recv2.at[source(i)], s2.at[i], r2.at[i], patch_0=source(i)).wait_recv()
+    seven = pl.ds(0, 7)
+    remote(send2.at[seven], recv2.at[seven], snd.at[4], rcv.at[0], patch_0=y).wait_recv()
     for h in range(HEADS):
         at_s[HEAD_DIM * h : HEAD_DIM * (h + 1), :] = recv2[h].astype(F32)[:HEAD_DIM]
     attn_t = at_s[...].astype(BF)
     pa_s[0] = attn_t
-    swap_a = remote(pa_s.at[0], pa_s.at[1], gs.at[1], gr.at[1], patch_1=other)
+    swap_a = remote(pa_s.at[0], pa_s.at[1], snd.at[5], rcv.at[1], patch_1=other)
     swap_a.start()
     output = dot(attn_t, w_s[...], 0, 0)
     token = lax.broadcasted_iota(jnp.int32, (ROWS, WIDTH), 0)
@@ -286,11 +303,9 @@
             [grad_attn[HEAD_DIM * h : HEAD_DIM * (h + 1)], jnp.zeros((8, ROWS), F32)], axis=0
         )
         send3[h] = block.astype(BF)
-    third = [None] * 8
     for i in FAR:
         to = lax.rem(y + i, 8)
-        third[i] = remote(send3.at[to], recv3.at[y], s3.at[i], r3.at[i], patch_0=to)
-        third[i].start()
+        remote(send3.at[to], recv3.at[y], snd.at[6], r3.at[i], patch_0=to).start()
     recv3[y] = send3[y]
 
     grad_t = (2.0 * error).T.astype(BF)
@@ -299,7 +314,7 @@
         for xx in range(nx):
             at = (2 * xx + half) * part
             g_s[half, part * xx : part * (xx + 1), :] = grad_t[at : at + part]
-    swap_g = remote(g_s.at[other], pg_s, gs.at[0], gr.at[0], patch_1=other)
+    swap_g = remote(g_s.at[other], pg_s, snd.at[7], rcv.at[2], patch_1=other)
     swap_g.start()
     squares = jnp.sum(error * error)
     cell = lax.broadcasted_iota(jnp.int32, (8, ROWS), 1)
@@ -307,29 +322,28 @@
         cell == 0, squares, jnp.where(cell == 1, length.astype(F32), 0.0)
     )
 
-    def stat_copies(stage, base, n, me, to):
-        return [
+    def stat_send(stage, base, n, me, to):
+        for i in range(1, n):
             remote(
                 stat_s.at[stage],
                 stat_s.at[base + i],
-                sts.at[base + i],
-                strr.at[base + i],
+                snd.at[8 + stage],
+                rcv.at[3 + stage],
                 **to(lax.rem(me + i, n)),
-            )
-            for i in range(1, n)
-        ]
-
-    def stat_sum(stage, base, n, copies):
-        for c in copies:
-            c.wait_recv()
+            ).start()
+
+    def stat_all(stage, base, n):
+        slots = stat_s.at[pl.ds(base + 1, n - 1)]
+        return remote(slots, slots, snd.at[8 + stage], rcv.at[3 + stage], patch_0=y)
+
+    def stat_sum(stage, base, n):
+        stat_all(stage, base, n).wait_recv()
         acc = stat_s[stage]
         for i in range(1, n):
             acc = acc + stat_s[base + i]
         return acc
 
-    stat_y = stat_copies(0, 3, 16, p, lambda t: {"patch_0": t // 2, "patch_1": lax.rem(t, 2)})
-    for c in stat_y:
-        c.start()
+    stat_send(0, 3, 16, p, lambda t: {"patch_0": t // 2, "patch_1": lax.rem(t, 2)})
     swap_a.wait_recv()
     swap_g.wait_recv()
     left = jnp.concatenate([g_s[k], pg_s[...]], axis=1)
@@ -337,16 +351,31 @@
     partial = dot(left, right, 1, 1)
     for xx in range(nx):
         xsend[xx] = partial[part * xx : part * (xx + 1)].astype(BF)
-    xcopies = [None] * nx
-    for i in range(1, nx):
-        to = lax.rem(x + i, nx)
-        xcopies[i] = remote(xsend.at[to], xrecv.at[i], xs.at[i], xr.at[i], dp_0=to)
-        xcopies[i].start()
-
-    def send_grad(s, rows, ssem, rsem):
-        i = lax.rem(s - y + 8, 8)
+    lo, hi = pl.ds(0, 80), pl.ds(80, 64)
+    up, down, across = lax.rem(x + 1, 4), lax.rem(x + 3, 4), lax.rem(x + 2, 4)
+    xring = [
+        remote(xsend.at[across, lo], xrel.at[lo], xs.at[0], xr.at[0], dp_0=up),
+        remote(xsend.at[across, hi], xrel.at[hi], xs.at[1], xr.at[1], dp_0=down),
+        remote(xsend.at[up, hi], xin.at[0, hi], xs.at[2], xr.at[2], dp_0=up),
+        remote(xsend.at[down, lo], xin.at[1, lo], xs.at[3], xr.at[3], dp_0=down),
+        remote(xacc.at[lo], xin.at[0, lo], xs.at[4], xr.at[4], dp_0=up),
+        remote(xacc.at[hi], xin.at[1, hi], xs.at[5], xr.at[5], dp_0=down),
+    ]
+    for c in xring[:4]:
+        c.start()
+
+    def x_relay():
+        for n, (rows, size, to) in enumerate(((0, 80, up), (80, 64, down))):
+            xring[n].wait_recv()
+            xacc[rows : rows + size, :] = (
+                xsend[to, rows : rows + size, :].astype(F32)
+                + xrel[rows : rows + size, :].astype(F32)
+            ).astype(BF)
+            xring[4 + n].start()
+
+    def send_grad(s, rows, n):
         return remote(
-            send4.at[s, rows], recv4.at[y, rows], ssem.at[i], rsem.at[i], patch_0=s
+            send4.at[s, rows], recv4.at[y, rows], snd.at[n], rcv.at[n], patch_0=s
         )
 
     qo = pl.ds(0, PAD)
@@ -354,7 +383,7 @@
 
     def third_in(s):
         i = lax.rem(y - s + 8, 8)
-        remote(send3.at[y], recv3.at[s], s3.at[i], r3.at[i], patch_0=s).wait_recv()
+        remote(send3.at[y], recv3.at[s], snd.at[6], r3.at[i], patch_0=y).wait_recv()
 
     for step_at in (0, 1, 3, 2):
         j = lax.rem(pair + step_at, 4)
@@ -377,19 +406,19 @@
         send4[2 * j, 0:PAD, :] = dq[:, :ROWS]
         send4[2 * j + 1, 0:PAD, :] = dq[:, ROWS:]
         if step_at:
-            send_grad(2 * j, qo, s4q, r4q).start()
-            send_grad(2 * j + 1, qo, s4q, r4q).start()
+            send_grad(2 * j, qo, 11).start()
+            send_grad(2 * j + 1, qo, 11).start()
         else:
-            send_grad(mate, qo, s4q, r4q).start()
-
-    stat_s[1] = stat_sum(0, 3, 16, stat_y)
-    stat_x = stat_copies(1, 19, nx, x, lambda t: {"dp_0": t})
-    for c in stat_x:
-        c.start()
+            send_grad(mate, qo, 11).start()
+        if step_at == 1:
+            x_relay()
+
+    stat_s[1] = stat_sum(0, 3, 16)
+    stat_send(1, 19, nx, x, lambda t: {"dp_0": t})
 
     def crossing(t):
         i = lax.rem(t - y + 8, 8)
-        return remote(dkv.at[other, t], drecv.at[t], dks.at[i], dkr.at[i], patch_1=other)
+        return remote(dkv.at[other, t], drecv.at[t], snd.at[13], dkr.at[i], patch_1=other)
 
     def join(t, away):
         crossing(t).wait_recv()
@@ -397,8 +426,34 @@
             dkv[k, t].astype(F32) + drecv[t].astype(F32)
         ).astype(BF)
         if away:
-            send_grad(t, kvo, s4, r4).start()
-
+            send_grad(t, kvo, 12).start()
+
+    cols = part // zh
+    active = z // zh == k
+
+    def x_done():
+        stat_s[2] = stat_sum(1, 19, nx)
+        stat_send(2, 19 + nx, nz, z, lambda t: {"dp_1": t})
+        for c in xring[2:]:
+            c.wait_recv()
+        total = xsend[x].astype(F32) + xin[0].astype(F32) + xin[1].astype(F32)
+        for j in range(zh):
+            zsend[j, 0:cols, :] = total[cols * j : cols * (j + 1)].astype(BF)
+        for j in range(zh):
+            to = zh * k + j
+            away = lax.rem(to - z + nz, nz)
+
+            @pl.when(to != z)
+            def _():
+                remote(
+                    zsend.at[j, zrows], zrecv.at[away, zrows], snd.at[14], rcv.at[6], dp_1=to
+                ).start()
+
+        @pl.when(active)
+        def _():
+            zrecv[0] = zsend[lax.rem(z, zh)]
+
+    zrows = pl.ds(0, ZROWS)
     order = FAR + (0,)
     for n, i in enumerate(order):
         t = lax.rem(y + i, 8)
@@ -411,78 +466,48 @@
             dkv[c, t, 0:PAD, :] = dk[:, ROWS * c : ROWS * (c + 1)]
             dkv[c, t, PAD : 2 * PAD, :] = dv[:, ROWS * c : ROWS * (c + 1)]
         crossing(t).start()
+        if n == XAT:
+            x_done()
         if n >= LAG:
             join(lax.rem(y + order[n - LAG], 8), order[n - LAG])
     for i in order[8 - LAG :]:
         join(lax.rem(y + i, 8), i)
 
-    for i in range(1, nx):
-        xcopies[i].wait_recv()
-    total = xsend[x].astype(F32)
-    for i in range(1, nx):
-        total = total + xrecv[i].astype(F32)
-    cols = part // zh
-    for j in range(zh):
-        zsend[j, 0:cols, :] = total[cols * j : cols * (j + 1)].astype(BF)
-    zcopies = [None] * zh
-    for j in range(zh):
-        to = zh * k + j
-        away = lax.rem(to - z + nz, nz)
-        zcopies[j] = remote(zsend.at[j], zrecv.at[away], zs.at[j], zr.at[away], dp_1=to)
-
-        @pl.when(to != z)
-        def _():
-            zcopies[j].start()
-
-    active = z // zh == k
+    recv4[y] = send4[y]
 
     @pl.when(active)
     def _():
-        zrecv[0] = zsend[lax.rem(z, zh)]
-
-    stat_s[2] = stat_sum(1, 19, nx, stat_x)
-    stat_z = stat_copies(2, 19 + nx, nz, z, lambda t: {"dp_1": t})
-    for c in stat_z:
-        c.start()
-    recv4[y] = send4[y]
-
-    def z_in(i):
-        return remote(zsend.at[0], zrecv.at[i], zs.at[0], zr.at[i], dp_1=z)
-
-    @pl.when(active)
-    def _():
-        for i in range(1, nz):
-            z_in(i).wait_recv()
+        z_all = zrecv.at[pl.ds(1, nz - 1), zrows]
+        remote(z_all, z_all, snd.at[14], rcv.at[6], patch_0=y).wait_recv()
         summed = zrecv[0].astype(F32)
         for i in range(1, nz):
             summed = summed + zrecv[i].astype(F32)
         for t in range(16):
-            ysend[t, 0:cols, 0:36] = summed[0:cols, 36 * t : 36 * (t + 1)]
-
-    def y_out(t):
-        return remote(
-            ysend.at[t], yrecv.at[y], ys.at[t], yr.at[y], patch_0=t // 2, patch_1=t % 2
-        )
+            piece = summed[:, 36 * t : 36 * (t + 1)]
+            ysend[t, :, 0:108] = jnp.concatenate(
+                [piece[0:16], piece[16:32], piece[32:48]], axis=1
+            )
 
     for t in range(16):
 
         @pl.when(active & (p != t))
         def _():
-            y_out(t).start()
+            remote(
+                ysend.at[t], yrecv.at[y], snd.at[15], rcv.at[7], patch_0=t // 2, patch_1=t % 2
+            ).start()
 
     @pl.when(active)
     def _():
         yrecv[y] = ysend[p]
 
-    acc = stat_sum(2, 19 + nx, nz, stat_z)
+    acc = stat_sum(2, 19 + nx, nz)
     count = acc[0:1, 1:2] / 16.0
     ratio = (nx * nz * 16.0 * ROWS) / count
     st_out[...] = acc[0:1, 0:1] / (count * WIDTH)
 
-    def grad_in(i, rows, ssem, rsem):
-        remote(
-            send4.at[y, rows], recv4.at[source(i), rows], ssem.at[i], rsem.at[i], patch_0=y
-        ).wait_recv()
+    def grad_all(rows, n):
+        blocks = recv4.at[seven, rows]
+        return remote(blocks, blocks, snd.at[n], rcv.at[n], patch_0=y)
 
     def emit(at, out):
         whole = jnp.concatenate(
@@ -494,51 +519,63 @@
         )
         out[0] = whole * ratio
 
-    for i in NEAR:
-        grad_in(i, qo, s4q, r4q)
+    grad_all(qo, 11).wait_recv()
     emit(0, dq_out)
-    for i in NEAR:
-        grad_in(i, kvo, s4, r4)
+    grad_all(kvo, 12).wait_recv()
     emit(1, dk_out)
     emit(2, dv_out)
 
-    for i in range(8):
-        here = active & (y == i)
-
-        @pl.when(jnp.logical_not(here))
-        def _():
-            remote(
-                ysend.at[0], yrecv.at[i], ys.at[0], yr.at[i], patch_0=y, patch_1=k
-            ).wait_recv()
+    def y_all(n):
+        blocks = yrecv.at[pl.ds(0, n)]
+        return remote(blocks, blocks, snd.at[15], rcv.at[7], patch_0=y)
+
+    @pl.when(active)
+    def _():
+        y_all(7).wait_recv()
+
+    @pl.when(jnp.logical_not(active))
+    def _():
+        y_all(8).wait_recv()
 
     final = yrecv[0]
     for i in range(1, 8):
         final = final + yrecv[i]
+    final = jnp.concatenate([final[:, 0:36], final[:, 36:72], final[:, 72:108]], axis=0)
     wg_out[...] = final.T[0:36, 0:36] * (ratio / (16.0 * ROWS))
 
-    for group in (first, first_v, third, xcopies):
-        for c in group[1:]:
-            c.wait_send()
-    for i in range(1, 8):
-        to = lax.rem(y + i, 8)
-        send_attn(to).wait_send()
-        send_grad(to, qo, s4q, r4q).wait_send()
-        send_grad(to, kvo, s4, r4).wait_send()
-    for i in range(8):
-        crossing(lax.rem(y + i, 8)).wait_send()
-    for c in passed + passed_v + [swap_a, swap_g] + stat_y + stat_x + stat_z:
+    def drain(ref, n):
+        remote(ref, ref, snd.at[n], rcv.at[0], patch_0=y).wait_send()
+
+    drain(send1.at[seven, qk], 0)
+    drain(send1.at[seven, vo], 1)
+    drain(send1.at[:, ko], 2)
+    drain(send1.at[:, vo], 3)
+    drain(send2.at[seven], 4)
+    drain(pa_s.at[0], 5)
+    drain(send3.at[seven], 6)
+    drain(pg_s, 7)
+    stat_all(0, 3, 16).wait_send()
+    stat_all(1, 19, nx).wait_send()
+    stat_all(2, 19 + nx, nz).wait_send()
+    drain(send4.at[seven, qo], 11)
+    drain(send4.at[seven, kvo], 12)
+    drain(drecv, 13)
+    for c in xring:
         c.wait_send()
-    for j in range(zh):
-
-        @pl.when(zh * k + j != z)
-        def _():
-            zcopies[j].wait_send()
-
-    for t in range(16):
-
-        @pl.when(active & (p != t))
-        def _():
-            y_out(t).wait_send()
+
+    @pl.when(k == 1)
+    def _():
+        relay_on(qk, 0, r1).wait_send()
+        relay_on(vo, 1, r1v).wait_send()
+
+    @pl.when(active)
+    def _():
+        drain(zsend.at[pl.ds(0, zh - 1), zrows], 14)
+        drain(ysend.at[pl.ds(0, 15)], 15)
+
+    @pl.when(jnp.logical_not(active))
+    def _():
+        drain(zsend.at[:, zrows], 14)
 
 
 def write_out(*refs):
@@ -585,15 +622,17 @@
         pltpu.VMEM((FEAT, ROWS), BF),
         pltpu.VMEM((2, FEAT, ROWS), BF),
         pltpu.VMEM((nx, part, FEAT), BF),
-        pltpu.VMEM((nx, part, FEAT), BF),
+        pltpu.VMEM((part, FEAT), BF),
+        pltpu.VMEM((part, FEAT), BF),
+        pltpu.VMEM((2, part, FEAT), BF),
         pltpu.VMEM((zh, 48, FEAT), BF),
         pltpu.VMEM((nz, 48, FEAT), BF),
-        pltpu.VMEM((16, 40, 128), F32),
-        pltpu.VMEM((8, 40, 128), F32),
+        pltpu.VMEM((16, 16, 128), F32),
+        pltpu.VMEM((8, 16, 128), F32),
         pltpu.VMEM((19 + nx + nz, 8, ROWS), F32),
+        pltpu.VMEM((3 * PAD, ROWS), BF),
     ]
-    sems = [6] + [8] * 18 + [2, 2, nx, nx, zh, nz, 16, 8]
-    sems += [19 + nx + nz] * 2
+    sems = [6, 16, 13, 8, 8, 2, 2, 8, 8, 8, 8, 6, 6]
     vmem = pl.BlockSpec(memory_space=pltpu.VMEM)
     hbm = pl.BlockSpec(memory_space=pltpu.HBM)
     wide = jax.ShapeDtypeStruct((1, FEAT, ROWS), F32)

time: 71.6 us -> 71.2 us (level); the launches traced: 70.6 us -> 71 us
  no operation moved by 1% of the time
where the time goes in v4:
time: 71.2 us; the launch traced here: 71 us
  Pallas kernels  69.8 us (98%)
  between operations  1.29 us (2%)
    pallas_call x1, Pallas kernels, step(): pl.pallas_call(functools.partial(body, nx, nz), out_shape=results, in_spe...  68.2 us
    pallas_call x1, Pallas kernels, step(): pl.pallas_call(write_out, out_shape=results, in_specs=[pl.BlockSpec(memor...  1.59 us

profile of v4, /device:TPU:1, one launch (start us, length us, event | category | flops | bytes accessed | tf_op | source)
XLA Modules:
  0.0 71.0 jit_solution(17937868278370847955)
XLA Ops:
  1.3 68.2 %shard_map.110 = (f32[1,576,128]{2,1,0:T(8,128)S(1)}, f32[1,576,128]{2,1,0:T(8,128)S(1)}, f32[1,576,128]{2,1,0:T(8,128)S(1)}, f32[36,36]{1,0:T(8,128)S(1)}, f32[1,1]{1,0:T(1,128)}) custom-call(bf16[1,576,128]{2,1,0:T(8,128)(2,1)} %bitcast.7, bf16[1,576,128]{2,1,0:T(8,128)(2,1)} %bitcast.8, bf16[1,576,128]{2,1,0:T(8,128)(2,1)} %bitcast.9, s32[1,128]{1,0:T(1,128)} %seg_hbm.1, ...), custom_call_target="tpu_custom_call" | custom-call | tf_op jit(solution)/shard_map/pallas_call | solution.py:647
  69.5 1.6 %shard_map.111 = (f32[1,576,128]{2,1,0:T(8,128)}, f32[1,576,128]{2,1,0:T(8,128)}, f32[1,576,128]{2,1,0:T(8,128)}, f32[36,36]{1,0:T(8,128)}, f32[1,1]{1,0:T(1,128)}) custom-call(f32[1,576,128]{2,1,0:T(8,128)S(1)} %get-tuple-element.15.refs_0_, f32[1,576,128]{2,1,0:T(8,128)S(1)} %get-tuple-element.16.refs_1_, f32[1,576,128]{2,1,0:T(8,128)S(1)} %get-tuple-element.17.refs_2_, ...), custom_call_target="tpu_custom_call" | custom-call | tf_op jit(solution)/shard_map/pallas_call | solution.py:665

commit v5 on v4

--- a/solution.py
+++ b/solution.py
@@ -21,9 +21,7 @@
 F32 = jnp.float32
 FAR = (4, 3, 5, 2, 6, 1, 7)
 NEAR = (1, 7, 2, 6, 3, 5, 4)
-LAG = 3
-XAT = 3
-ZROWS = 48
+XAT = 2
 MASK = 2.0**50
 
 
@@ -82,14 +80,14 @@
     ysend,
     yrecv,
     stat_s,
-    relay,
+    s_s,
+    top_s,
+    acc_s,
     load_sem,
     snd,
     rcv,
     r1,
     r1v,
-    rls,
-    rlr,
     d1r,
     d1vr,
     r3,
@@ -157,48 +155,24 @@
         for h in range(HEADS):
             block = jnp.concatenate([whole[HEAD_DIM * h : HEAD_DIM * (h + 1)], extra], axis=0)
             send1[h, PAD * at : PAD * (at + 1), :] = block.astype(BF)
-    recv1[p] = send1[y]
-
+    recv1[0, y] = send1[y]
+
+    recv3[...] = jnp.zeros_like(recv3)
     pl.semaphore_wait(barrier, 15 + (nx - 1) + (nz - 1))
 
     qk = pl.ds(0, 2 * PAD)
     ko = pl.ds(PAD, PAD)
     vo = pl.ds(2 * PAD, PAD)
 
-    two_on = lax.rem(y + 2, 8)
-
     def spread(rows, n, rsem):
         for i in FAR:
             h = lax.rem(y + i, 8)
-            direct = remote(
-                send1.at[h, rows], recv1.at[p, rows], snd.at[n], rsem.at[i], patch_0=h
-            )
-            if i != 4:
-                direct.start()
-                continue
-
-            @pl.when(k == 0)
-            def _():
-                direct.start()
-
-            @pl.when(k == 1)
-            def _():
-                remote(
-                    send1.at[h, rows], relay.at[rows], snd.at[n], rlr.at[n], patch_0=two_on
-                ).start()
-
-    def relay_on(rows, n, rsem):
-        at = recv1.at[2 * lax.rem(y + 6, 8) + k, rows]
-        return remote(relay.at[rows], at, rls.at[n], rsem.at[4], patch_0=two_on)
-
-    def relay_in(rows, n, rsem):
-        @pl.when(k == 1)
-        def _():
-            remote(relay.at[rows], relay.at[rows], rls.at[n], rlr.at[n], patch_0=y).wait_recv()
-            relay_on(rows, n, rsem).start()
+            remote(
+                send1.at[h, rows], recv1.at[0, y, rows], snd.at[n], rsem.at[i], patch_0=h
+            ).start()
 
     def block_in(i, rows, rsem):
-        b = recv1.at[2 * source(i) + k, rows]
+        b = recv1.at[0, source(i), rows]
         remote(b, b, snd.at[0], rsem.at[i], patch_0=y).wait_recv()
 
     spread(qk, 0, r1)
@@ -208,56 +182,82 @@
         return lax.rem(y - i + 8, 8)
 
     def pass_on(i, rows, n, rsem):
-        ref = recv1.at[2 * source(i) + k, rows]
-        return remote(ref, ref, snd.at[n], rsem.at[i], patch_1=other)
-
-    def token_major(dst, b, part, at):
-        at = pl.ds(pl.multiple_of(at * ROWS, ROWS), ROWS)
-        dst[at, :] = recv1[b, PAD * part : PAD * (part + 1), :].astype(F32).T.astype(BF)
+        return remote(
+            recv1.at[0, source(i), rows],
+            recv1.at[1, source(i), rows],
+            snd.at[n],
+            rsem.at[i],
+            patch_1=other,
+        )
+
+    def token_major(dst, c, src, part):
+        at = pl.ds(pl.multiple_of((8 * c + src) * ROWS, ROWS), ROWS)
+        dst[at, :] = recv1[c, src, PAD * part : PAD * (part + 1), :].astype(F32).T.astype(BF)
 
     passed = [pass_on(i, ko, 2, d1r) for i in range(8)]
     passed_v = [pass_on(i, vo, 3, d1vr) for i in range(8)]
     passed[0].start()
     passed_v[0].start()
-    token_major(ktok, p, 1, p)
+    token_major(ktok, 0, y, 1)
     for i in NEAR:
-        if i == 2:
-            relay_in(qk, 0, r1)
         block_in(i, qk, r1)
         passed[i].start()
-        b = 2 * source(i) + k
-        token_major(ktok, b, 1, b)
-    relay_in(vo, 1, r1v)
-    for i in (0,) + NEAR:
-        passed[i].wait_recv()
-        b = 2 * source(i) + other
-        token_major(ktok, b, 1, b)
+        token_major(ktok, 0, source(i), 1)
 
     factor = scale * math.log2(math.e)
     pair = y // 2
     mate = y + 1 - 2 * lax.rem(y, 2)
-
-    def forward(j, carry):
-        queries = jnp.concatenate([recv1[4 * j + k, 0:PAD, :], recv1[4 * j + 2 + k, 0:PAD, :]], axis=1)
-        scores = dot(ktok[...], queries, 1, 0)
-        top = jnp.max(scores, axis=0, keepdims=True)
-        p_s[j] = jnp.exp2((scores - top) * factor).astype(BF)
+    half = 8 * ROWS
+
+    def queries(j):
+        return jnp.concatenate([recv1[0, 2 * j, 0:PAD, :], recv1[0, 2 * j + 1, 0:PAD, :]], axis=1)
+
+    def forward_own(j, carry):
+        scores = dot(ktok[0:half, :], queries(j), 1, 0)
+        s_s[j] = scores
+        top_s[j] = jnp.broadcast_to(jnp.max(scores, axis=0, keepdims=True), (8, 2 * ROWS))
         return carry
 
-    lax.fori_loop(0, 4, forward, 0)
+    lax.fori_loop(0, 4, forward_own, 0)
+    for i in (0,) + NEAR:
+        passed[i].wait_recv()
+        token_major(ktok, 1, source(i), 1)
+
+    def forward_other(j, carry):
+        scores = dot(ktok[half : 2 * half, :], queries(j), 1, 0)
+        top = jnp.maximum(top_s[j, 0:1, :], jnp.max(scores, axis=0, keepdims=True))
+        p_s[j, half : 2 * half, :] = jnp.exp2((scores - top) * factor).astype(BF)
+        p_s[j, 0:half, :] = jnp.exp2((s_s[j] - top) * factor).astype(BF)
+        return carry
+
+    lax.fori_loop(0, 4, forward_other, 0)
     for i in NEAR:
         block_in(i, vo, r1v)
         passed_v[i].start()
+
+    def lanes(c, part):
+        return jnp.concatenate(
+            [recv1[c, src, PAD * part : PAD * (part + 1), :] for src in range(8)], axis=1
+        )
+
+    def values_own(j, carry):
+        acc_s[j] = dot(lanes(0, 2), p_s[j, 0:half, :], 1, 0)
+        return carry
+
+    lax.fori_loop(0, 4, values_own, 0)
     for i in (0,) + NEAR:
         passed_v[i].wait_recv()
 
+    head = pl.ds(0, HEAD_DIM)
+
     def send_attn(s):
-        return remote(send2.at[s], recv2.at[y], snd.at[4], rcv.at[0], patch_0=s)
+        return remote(
+            send2.at[s, head], recv2.at[y, head], snd.at[4], rcv.at[0], patch_0=s
+        )
 
     for step_at in (2, 1, 3, 0):
         j = lax.rem(pair + step_at, 4)
-        values = jnp.concatenate([recv1[b, 2 * PAD : 3 * PAD, :] for b in range(16)], axis=1)
-        accum = dot(values, p_s[j], 1, 0)
+        accum = acc_s[j] + dot(lanes(1, 2), p_s[j, half : 2 * half, :], 1, 0)
         rinv = 1.0 / accum[HEAD_DIM : HEAD_DIM + 1, :]
         rinv_s[j] = jnp.broadcast_to(rinv, (8, 2 * ROWS))
         attn = (accum * rinv).astype(BF)
@@ -270,22 +270,20 @@
             send_attn(mate).start()
     recv2[y] = send2[y]
 
-    def backward_layouts(b, carry):
-        token_major(vtok, b, 2, b)
+    def backward_layouts(src, carry):
+        token_major(vtok, 0, src, 2)
+        token_major(vtok, 1, src, 2)
+        token_major(qtok, 0, src, 0)
         return carry
 
-    lax.fori_loop(0, 16, backward_layouts, 0)
-
-    def query_layouts(src, carry):
-        token_major(qtok, 2 * src + k, 0, src)
-        return carry
-
-    lax.fori_loop(0, 8, query_layouts, 0)
+    lax.fori_loop(0, 8, backward_layouts, 0)
 
     loads[4].wait()
     loads[5].wait()
     seven = pl.ds(0, 7)
-    remote(send2.at[seven], recv2.at[seven], snd.at[4], rcv.at[0], patch_0=y).wait_recv()
+    remote(
+        send2.at[seven, head], recv2.at[seven, head], snd.at[4], rcv.at[0], patch_0=y
+    ).wait_recv()
     for h in range(HEADS):
         at_s[HEAD_DIM * h : HEAD_DIM * (h + 1), :] = recv2[h].astype(F32)[:HEAD_DIM]
     attn_t = at_s[...].astype(BF)
@@ -297,7 +295,15 @@
     live = p * ROWS + token < length
     error = jnp.where(live, output - t_s[0].astype(F32), 0.0)
     grad_out = (2.0 * error).astype(BF)
-    grad_attn = dot(w_s[...], grad_out, 1, 1)
+    grad_t = (2.0 * error).T.astype(BF)
+    part = WIDTH // (2 * nx)
+    for zhalf in range(2):
+        for xx in range(nx):
+            at = (2 * xx + zhalf) * part
+            g_s[zhalf, part * xx : part * (xx + 1), :] = grad_t[at : at + part]
+    swap_g = remote(g_s.at[other], pg_s, snd.at[7], rcv.at[2], patch_1=other)
+    swap_g.start()
+    grad_attn = dot(w_s[...], grad_t, 1, 0)
     for h in range(HEADS):
         block = jnp.concatenate(
             [grad_attn[HEAD_DIM * h : HEAD_DIM * (h + 1)], jnp.zeros((8, ROWS), F32)], axis=0
@@ -305,17 +311,11 @@
         send3[h] = block.astype(BF)
     for i in FAR:
         to = lax.rem(y + i, 8)
-        remote(send3.at[to], recv3.at[y], snd.at[6], r3.at[i], patch_0=to).start()
-    recv3[y] = send3[y]
-
-    grad_t = (2.0 * error).T.astype(BF)
-    part = WIDTH // (2 * nx)
-    for half in range(2):
-        for xx in range(nx):
-            at = (2 * xx + half) * part
-            g_s[half, part * xx : part * (xx + 1), :] = grad_t[at : at + part]
-    swap_g = remote(g_s.at[other], pg_s, snd.at[7], rcv.at[2], patch_1=other)
-    swap_g.start()
+        remote(
+            send3.at[to, head], recv3.at[y, head], snd.at[6], r3.at[i], patch_0=to
+        ).start()
+    recv3[y, 0:HEAD_DIM, :] = send3[y, 0:HEAD_DIM, :]
+
     squares = jnp.sum(error * error)
     cell = lax.broadcasted_iota(jnp.int32, (8, ROWS), 1)
     stat_s[0] = jnp.where(
@@ -350,8 +350,12 @@
     right = jnp.concatenate([pa_s[0], pa_s[1]], axis=1)
     partial = dot(left, right, 1, 1)
     for xx in range(nx):
-        xsend[xx] = partial[part * xx : part * (xx + 1)].astype(BF)
-    lo, hi = pl.ds(0, 80), pl.ds(80, 64)
+        chunk = partial[part * xx : part * (xx + 1)]
+        rest = jnp.concatenate([chunk[: part // 2, 512:], chunk[part // 2 :, 512:]], axis=1)
+        for g in range(4):
+            xsend[xx, part * g : part * (g + 1), :] = chunk[:, ROWS * g : ROWS * (g + 1)].astype(BF)
+        xsend[xx, 4 * part :, :] = jnp.concatenate([rest, jnp.zeros((8, ROWS), F32)], axis=0).astype(BF)
+    lo, hi = pl.ds(0, 336), pl.ds(336, 320)
     up, down, across = lax.rem(x + 1, 4), lax.rem(x + 3, 4), lax.rem(x + 2, 4)
     xring = [
         remote(xsend.at[across, lo], xrel.at[lo], xs.at[0], xr.at[0], dp_0=up),
@@ -365,7 +369,7 @@
         c.start()
 
     def x_relay():
-        for n, (rows, size, to) in enumerate(((0, 80, up), (80, 64, down))):
+        for n, (rows, size, to) in enumerate(((0, 336, up), (336, 320, down))):
             xring[n].wait_recv()
             xacc[rows : rows + size, :] = (
                 xsend[to, rows : rows + size, :].astype(F32)
@@ -378,12 +382,14 @@
             send4.at[s, rows], recv4.at[y, rows], snd.at[n], rcv.at[n], patch_0=s
         )
 
-    qo = pl.ds(0, PAD)
-    kvo = pl.ds(PAD, 2 * PAD)
+    qo = pl.ds(0, HEAD_DIM)
+    kvo = pl.ds(PAD, 2 * HEAD_DIM)
 
     def third_in(s):
         i = lax.rem(y - s + 8, 8)
-        remote(send3.at[y], recv3.at[s], snd.at[6], r3.at[i], patch_0=y).wait_recv()
+        remote(
+            send3.at[y, head], recv3.at[s, head], snd.at[6], r3.at[i], patch_0=y
+        ).wait_recv()
 
     for step_at in (0, 1, 3, 2):
         j = lax.rem(pair + step_at, 4)
@@ -401,7 +407,7 @@
         dprobs = dot(vtok[...], folded, 1, 0)
         dscores = (p_s[j].astype(F32) * (dprobs - delta)).astype(BF)
         ds_s[j] = dscores
-        keys = jnp.concatenate([recv1[b, PAD : 2 * PAD, :] for b in range(16)], axis=1)
+        keys = jnp.concatenate([lanes(0, 1), lanes(1, 1)], axis=1)
         dq = (dot(keys, dscores, 1, 0) * scale).astype(BF)
         send4[2 * j, 0:PAD, :] = dq[:, :ROWS]
         send4[2 * j + 1, 0:PAD, :] = dq[:, ROWS:]
@@ -416,17 +422,17 @@
     stat_s[1] = stat_sum(0, 3, 16)
     stat_send(1, 19, nx, x, lambda t: {"dp_0": t})
 
-    def crossing(t):
-        i = lax.rem(t - y + 8, 8)
-        return remote(dkv.at[other, t], drecv.at[t], snd.at[13], dkr.at[i], patch_1=other)
-
-    def join(t, away):
-        crossing(t).wait_recv()
-        send4[t, PAD : 3 * PAD, :] = (
-            dkv[k, t].astype(F32) + drecv[t].astype(F32)
-        ).astype(BF)
-        if away:
-            send_grad(t, kvo, 12).start()
+    def crossing(u):
+        two = pl.ds(2 * u, 2)
+        return remote(dkv.at[two], drecv.at[two], snd.at[13], dkr.at[u], patch_1=other)
+
+    def key_grads(c, u):
+        at = pl.ds(pl.multiple_of((8 * c + 2 * u) * ROWS, 2 * ROWS), 2 * ROWS)
+        ds_rows = jnp.concatenate([ds_s[j, at, :] for j in range(4)], axis=1)
+        p_rows = jnp.concatenate([p_s[j, at, :] for j in range(4)], axis=1)
+        dk = (dot(ds_rows, qtok[...], 1, 0) * scale).T
+        dv = dot(p_rows, dtok[...], 1, 0).T
+        return jnp.concatenate([dk[:HEAD_DIM], dv[:HEAD_DIM]], axis=0)
 
     cols = part // zh
     active = z // zh == k
@@ -438,7 +444,14 @@
             c.wait_recv()
         total = xsend[x].astype(F32) + xin[0].astype(F32) + xin[1].astype(F32)
         for j in range(zh):
-            zsend[j, 0:cols, :] = total[cols * j : cols * (j + 1)].astype(BF)
+            rest = total[4 * part + cols * (j % 2) : 4 * part + cols * (j % 2 + 1)]
+            rest = rest[:, 64 * (j // 2) : 64 * (j // 2 + 1)]
+            rows = [total[part * g + cols * j : part * g + cols * (j + 1)] for g in range(4)]
+            rows += [
+                jnp.concatenate([rest[: cols // 2], rest[cols // 2 :]], axis=1),
+                jnp.zeros((14, ROWS), F32),
+            ]
+            zsend[j] = jnp.concatenate(rows, axis=0).astype(BF)
         for j in range(zh):
             to = zh * k + j
             away = lax.rem(to - z + nz, nz)
@@ -446,42 +459,50 @@
             @pl.when(to != z)
             def _():
                 remote(
-                    zsend.at[j, zrows], zrecv.at[away, zrows], snd.at[14], rcv.at[6], dp_1=to
+                    zsend.at[j], zrecv.at[away], snd.at[14], rcv.at[6], dp_1=to
                 ).start()
 
         @pl.when(active)
         def _():
             zrecv[0] = zsend[lax.rem(z, zh)]
 
-    zrows = pl.ds(0, ZROWS)
-    order = FAR + (0,)
-    for n, i in enumerate(order):
-        t = lax.rem(y + i, 8)
-        at = pl.ds(pl.multiple_of(t * 2 * ROWS, 2 * ROWS), 2 * ROWS)
-        ds_rows = jnp.concatenate([ds_s[j, at, :] for j in range(4)], axis=1)
-        p_rows = jnp.concatenate([p_s[j, at, :] for j in range(4)], axis=1)
-        dk = (dot(ds_rows, qtok[...], 1, 0) * scale).T.astype(BF)
-        dv = dot(p_rows, dtok[...], 1, 0).T.astype(BF)
+    for step_at in (2, 1, 3, 0):
+        u = lax.rem(pair + step_at, 4)
+        both = key_grads(1, u).astype(BF)
+        dkv[2 * u] = both[:, :ROWS]
+        dkv[2 * u + 1] = both[:, ROWS:]
+        crossing(u).start()
+    for step_at in (2, 1, 3, 0):
+        u = lax.rem(pair + step_at, 4)
+        both = key_grads(0, u)
+        crossing(u).wait_recv()
         for c in range(2):
-            dkv[c, t, 0:PAD, :] = dk[:, ROWS * c : ROWS * (c + 1)]
-            dkv[c, t, PAD : 2 * PAD, :] = dv[:, ROWS * c : ROWS * (c + 1)]
-        crossing(t).start()
-        if n == XAT:
+            mine = both[:, ROWS * c : ROWS * (c + 1)]
+            send4[2 * u + c, PAD:, :] = (mine + drecv[2 * u + c].astype(F32)).astype(BF)
+        if step_at:
+            send_grad(2 * u, kvo, 12).start()
+            send_grad(2 * u + 1, kvo, 12).start()
+        else:
+            send_grad(mate, kvo, 12).start()
+        if step_at == XAT:
             x_done()
-        if n >= LAG:
-            join(lax.rem(y + order[n - LAG], 8), order[n - LAG])
-    for i in order[8 - LAG :]:
-        join(lax.rem(y + i, 8), i)
 
     recv4[y] = send4[y]
 
     @pl.when(active)
     def _():
-        z_all = zrecv.at[pl.ds(1, nz - 1), zrows]
+        z_all = zrecv.at[pl.ds(1, nz - 1)]
         remote(z_all, z_all, snd.at[14], rcv.at[6], patch_0=y).wait_recv()
         summed = zrecv[0].astype(F32)
         for i in range(1, nz):
             summed = summed + zrecv[i].astype(F32)
+        rest = summed[4 * cols : 4 * cols + cols // 2]
+        summed = jnp.concatenate(
+            [summed[cols * g : cols * (g + 1)] for g in range(4)]
+            + [jnp.concatenate([rest[:, :64], rest[:, 64:]], axis=0)],
+            axis=1,
+        )
+        summed = jnp.concatenate([summed, jnp.zeros((48 - cols, FEAT), F32)], axis=0)
         for t in range(16):
             piece = summed[:, 36 * t : 36 * (t + 1)]
             ysend[t, :, 0:108] = jnp.concatenate(
@@ -509,12 +530,11 @@
         blocks = recv4.at[seven, rows]
         return remote(blocks, blocks, snd.at[n], rcv.at[n], patch_0=y)
 
-    def emit(at, out):
+    def emit(start, out):
+        rows = slice(start // 16 * 16, (start // 16 + 5) * 16)
+        skip = start % 16
         whole = jnp.concatenate(
-            [
-                recv4[h, PAD * at : PAD * (at + 1), :].astype(F32)[:HEAD_DIM]
-                for h in range(HEADS)
-            ],
+            [recv4[h, rows, :].astype(F32)[skip : skip + HEAD_DIM] for h in range(HEADS)],
             axis=0,
         )
         out[0] = whole * ratio
@@ -522,8 +542,8 @@
     grad_all(qo, 11).wait_recv()
     emit(0, dq_out)
     grad_all(kvo, 12).wait_recv()
-    emit(1, dk_out)
-    emit(2, dv_out)
+    emit(PAD, dk_out)
+    emit(PAD + HEAD_DIM, dv_out)
 
     def y_all(n):
         blocks = yrecv.at[pl.ds(0, n)]
@@ -550,9 +570,9 @@
     drain(send1.at[seven, vo], 1)
     drain(send1.at[:, ko], 2)
     drain(send1.at[:, vo], 3)
-    drain(send2.at[seven], 4)
+    drain(send2.at[seven, head], 4)
     drain(pa_s.at[0], 5)
-    drain(send3.at[seven], 6)
+    drain(send3.at[seven, head], 6)
     drain(pg_s, 7)
     stat_all(0, 3, 16).wait_send()
     stat_all(1, 19, nx).wait_send()
@@ -563,19 +583,14 @@
     for c in xring:
         c.wait_send()
 
-    @pl.when(k == 1)
-    def _():
-        relay_on(qk, 0, r1).wait_send()
-        relay_on(vo, 1, r1v).wait_send()
-
     @pl.when(active)
     def _():
-        drain(zsend.at[pl.ds(0, zh - 1), zrows], 14)
+        drain(zsend.at[pl.ds(0, zh - 1)], 14)
         drain(ysend.at[pl.ds(0, 15)], 15)
 
     @pl.when(jnp.logical_not(active))
     def _():
-        drain(zsend.at[:, zrows], 14)
+        drain(zsend, 14)
 
 
 def write_out(*refs):
@@ -601,7 +616,7 @@
         pltpu.VMEM((FEAT, WIDTH), BF),
         pltpu.VMEM((1, ROWS, WIDTH), BF),
         pltpu.VMEM((8, 3 * PAD, ROWS), BF),
-        pltpu.VMEM((16, 3 * PAD, ROWS), BF),
+        pltpu.VMEM((2, 8, 3 * PAD, ROWS), BF),
         pltpu.VMEM((2048, PAD), BF),
         pltpu.VMEM((2048, PAD), BF),
         pltpu.VMEM((1024, PAD), BF),
@@ -614,25 +629,27 @@
         pltpu.VMEM((FEAT, ROWS), F32),
         pltpu.VMEM((8, PAD, ROWS), BF),
         pltpu.VMEM((8, PAD, ROWS), BF),
-        pltpu.VMEM((2, 8, 2 * PAD, ROWS), BF),
-        pltpu.VMEM((8, 2 * PAD, ROWS), BF),
-        pltpu.VMEM((8, 3 * PAD, ROWS), BF),
-        pltpu.VMEM((8, 3 * PAD, ROWS), BF),
+        pltpu.VMEM((8, 2 * HEAD_DIM, ROWS), BF),
+        pltpu.VMEM((8, 2 * HEAD_DIM, ROWS), BF),
+        pltpu.VMEM((8, PAD + 2 * HEAD_DIM, ROWS), BF),
+        pltpu.VMEM((8, PAD + 2 * HEAD_DIM, ROWS), BF),
         pltpu.VMEM((2, FEAT, ROWS), BF),
         pltpu.VMEM((FEAT, ROWS), BF),
         pltpu.VMEM((2, FEAT, ROWS), BF),
-        pltpu.VMEM((nx, part, FEAT), BF),
-        pltpu.VMEM((part, FEAT), BF),
-        pltpu.VMEM((part, FEAT), BF),
-        pltpu.VMEM((2, part, FEAT), BF),
-        pltpu.VMEM((zh, 48, FEAT), BF),
-        pltpu.VMEM((nz, 48, FEAT), BF),
+        pltpu.VMEM((nx, 656, ROWS), BF),
+        pltpu.VMEM((656, ROWS), BF),
+        pltpu.VMEM((656, ROWS), BF),
+        pltpu.VMEM((2, 656, ROWS), BF),
+        pltpu.VMEM((zh, 176, ROWS), BF),
+        pltpu.VMEM((nz, 176, ROWS), BF),
         pltpu.VMEM((16, 16, 128), F32),
         pltpu.VMEM((8, 16, 128), F32),
         pltpu.VMEM((19 + nx + nz, 8, ROWS), F32),
-        pltpu.VMEM((3 * PAD, ROWS), BF),
+        pltpu.VMEM((4, 1024, 256), F32),
+        pltpu.VMEM((4, 8, 256), F32),
+        pltpu.VMEM((4, PAD, 256), F32),
     ]
-    sems = [6, 16, 13, 8, 8, 2, 2, 8, 8, 8, 8, 6, 6]
+    sems = [6, 16, 13, 8, 8, 8, 8, 8, 4, 6, 6]
     vmem = pl.BlockSpec(memory_space=pltpu.VMEM)
     hbm = pl.BlockSpec(memory_space=pltpu.HBM)
     wide = jax.ShapeDtypeStruct((1, FEAT, ROWS), F32)

time: 71.2 us -> 68.3 us (0.959)
  Pallas kernels: 69.8 us -> 66.9 us
    pallas_call x1, Pallas kernels: 68.2 us -> 65.3 us  [step(): pl.pallas_call(functools.partial(body, nx, nz), out_shape=results, in_spe...]
where the time goes in v5:
time: 68.3 us; the launch traced here: 68.2 us
  Pallas kernels  66.9 us (98%)
  between operations  1.29 us (2%)
    pallas_call x1, Pallas kernels, step(): pl.pallas_call(functools.partial(body, nx, nz), out_shape=results, in_spe...  65.3 us
    pallas_call x1, Pallas kernels, step(): pl.pallas_call(write_out, out_shape=results, in_specs=[pl.BlockSpec(memor...  1.59 us

profile of v5, /device:TPU:1, one launch (start us, length us, event | category | flops | bytes accessed | tf_op | source)
XLA Modules:
  0.0 68.2 jit_solution(7201305688695568612)
XLA Ops:
  1.3 65.3 %shard_map.110 = (f32[1,576,128]{2,1,0:T(8,128)S(1)}, f32[1,576,128]{2,1,0:T(8,128)S(1)}, f32[1,576,128]{2,1,0:T(8,128)S(1)}, f32[36,36]{1,0:T(8,128)S(1)}, f32[1,1]{1,0:T(1,128)}) custom-call(bf16[1,576,128]{2,1,0:T(8,128)(2,1)} %bitcast.7, bf16[1,576,128]{2,1,0:T(8,128)(2,1)} %bitcast.8, bf16[1,576,128]{2,1,0:T(8,128)(2,1)} %bitcast.9, s32[1,128]{1,0:T(1,128)} %seg_hbm.1, ...), custom_call_target="tpu_custom_call" | custom-call | tf_op jit(solution)/shard_map/pallas_call | solution.py:664
  66.6 1.6 %shard_map.111 = (f32[1,576,128]{2,1,0:T(8,128)}, f32[1,576,128]{2,1,0:T(8,128)}, f32[1,576,128]{2,1,0:T(8,128)}, f32[36,36]{1,0:T(8,128)}, f32[1,1]{1,0:T(1,128)}) custom-call(f32[1,576,128]{2,1,0:T(8,128)S(1)} %get-tuple-element.15.refs_0_, f32[1,576,128]{2,1,0:T(8,128)S(1)} %get-tuple-element.16.refs_1_, f32[1,576,128]{2,1,0:T(8,128)S(1)} %get-tuple-element.17.refs_2_, ...), custom_call_target="tpu_custom_call" | custom-call | tf_op jit(solution)/shard_map/pallas_call | solution.py:682

commit v6 on v5

--- a/solution.py
+++ b/solution.py
@@ -21,7 +21,6 @@
 F32 = jnp.float32
 FAR = (4, 3, 5, 2, 6, 1, 7)
 NEAR = (1, 7, 2, 6, 3, 5, 4)
-XAT = 2
 MASK = 2.0**50
 
 
@@ -89,7 +88,6 @@
     r1,
     r1v,
     d1r,
-    d1vr,
     r3,
     dkr,
     xs,
@@ -186,7 +184,7 @@
             recv1.at[0, source(i), rows],
             recv1.at[1, source(i), rows],
             snd.at[n],
-            rsem.at[i],
+            rsem,
             patch_1=other,
         )
 
@@ -194,15 +192,27 @@
         at = pl.ds(pl.multiple_of((8 * c + src) * ROWS, ROWS), ROWS)
         dst[at, :] = recv1[c, src, PAD * part : PAD * (part + 1), :].astype(F32).T.astype(BF)
 
-    passed = [pass_on(i, ko, 2, d1r) for i in range(8)]
-    passed_v = [pass_on(i, vo, 3, d1vr) for i in range(8)]
+    def pass_keys(i):
+        at = pl.multiple_of(source(i) * ROWS, ROWS)
+        return remote(
+            ktok.at[pl.ds(at, ROWS)],
+            ktok.at[pl.ds(8 * ROWS + at, ROWS)],
+            snd.at[16],
+            d1r.at[i],
+            patch_1=other,
+        )
+
+    passed = [pass_on(i, ko, 2, rcv.at[8]) for i in range(8)]
+    passed_v = [pass_on(i, vo, 3, rcv.at[9]) for i in range(8)]
+    token_major(ktok, 0, y, 1)
+    pass_keys(0).start()
     passed[0].start()
     passed_v[0].start()
-    token_major(ktok, 0, y, 1)
     for i in NEAR:
         block_in(i, qk, r1)
+        token_major(ktok, 0, source(i), 1)
+        pass_keys(i).start()
         passed[i].start()
-        token_major(ktok, 0, source(i), 1)
 
     factor = scale * math.log2(math.e)
     pair = y // 2
@@ -220,8 +230,7 @@
 
     lax.fori_loop(0, 4, forward_own, 0)
     for i in (0,) + NEAR:
-        passed[i].wait_recv()
-        token_major(ktok, 1, source(i), 1)
+        pass_keys(i).wait_recv()
 
     def forward_other(j, carry):
         scores = dot(ktok[half : 2 * half, :], queries(j), 1, 0)
@@ -245,8 +254,8 @@
         return carry
 
     lax.fori_loop(0, 4, values_own, 0)
-    for i in (0,) + NEAR:
-        passed_v[i].wait_recv()
+    crossed = recv1.at[1, :, vo]
+    remote(crossed, crossed, snd.at[3], rcv.at[9], patch_0=y).wait_recv()
 
     head = pl.ds(0, HEAD_DIM)
 
@@ -316,34 +325,6 @@
         ).start()
     recv3[y, 0:HEAD_DIM, :] = send3[y, 0:HEAD_DIM, :]
 
-    squares = jnp.sum(error * error)
-    cell = lax.broadcasted_iota(jnp.int32, (8, ROWS), 1)
-    stat_s[0] = jnp.where(
-        cell == 0, squares, jnp.where(cell == 1, length.astype(F32), 0.0)
-    )
-
-    def stat_send(stage, base, n, me, to):
-        for i in range(1, n):
-            remote(
-                stat_s.at[stage],
-                stat_s.at[base + i],
-                snd.at[8 + stage],
-                rcv.at[3 + stage],
-                **to(lax.rem(me + i, n)),
-            ).start()
-
-    def stat_all(stage, base, n):
-        slots = stat_s.at[pl.ds(base + 1, n - 1)]
-        return remote(slots, slots, snd.at[8 + stage], rcv.at[3 + stage], patch_0=y)
-
-    def stat_sum(stage, base, n):
-        stat_all(stage, base, n).wait_recv()
-        acc = stat_s[stage]
-        for i in range(1, n):
-            acc = acc + stat_s[base + i]
-        return acc
-
-    stat_send(0, 3, 16, p, lambda t: {"patch_0": t // 2, "patch_1": lax.rem(t, 2)})
     swap_a.wait_recv()
     swap_g.wait_recv()
     left = jnp.concatenate([g_s[k], pg_s[...]], axis=1)
@@ -376,6 +357,37 @@
                 + xrel[rows : rows + size, :].astype(F32)
             ).astype(BF)
             xring[4 + n].start()
+
+    squares = jnp.sum(error * error)
+    cell = lax.broadcasted_iota(jnp.int32, (8, ROWS), 1)
+    stat_s[0] = jnp.where(
+        cell == 0, squares, jnp.where(cell == 1, length.astype(F32), 0.0)
+    )
+
+    def stat_send(stage, base, n, me, to):
+        for i in range(1, n):
+            remote(
+                stat_s.at[stage],
+                stat_s.at[base + i],
+                snd.at[8 + stage],
+                rcv.at[3 + stage],
+                **to(lax.rem(me + i, n)),
+            ).start()
+
+    def stat_all(stage, base, n):
+        slots = stat_s.at[pl.ds(base + 1, n - 1)]
+        return remote(slots, slots, snd.at[8 + stage], rcv.at[3 + stage], patch_0=y)
+
+    def stat_sum(stage, base, n):
+        stat_all(stage, base, n).wait_recv()
+        acc = stat_s[stage]
+        for i in range(1, n):
+            acc = acc + stat_s[base + i]
+        return acc
+
+    stat_send(0, 3, 16, p, lambda t: {"patch_0": t // 2, "patch_1": lax.rem(t, 2)})
+    crossed = recv1.at[1, :, ko]
+    remote(crossed, crossed, snd.at[2], rcv.at[8], patch_0=y).wait_recv()
 
     def send_grad(s, rows, n):
         return remote(
@@ -452,7 +464,9 @@
                 jnp.zeros((14, ROWS), F32),
             ]
             zsend[j] = jnp.concatenate(rows, axis=0).astype(BF)
-        for j in range(zh):
+        start = z + jnp.where(active, 2, 0)
+        for step_at in (0, 1, 3, 2):
+            j = lax.rem(start + step_at, zh)
             to = zh * k + j
             away = lax.rem(to - z + nz, nz)
 
@@ -466,13 +480,14 @@
         def _():
             zrecv[0] = zsend[lax.rem(z, zh)]
 
-    for step_at in (2, 1, 3, 0):
+    def other_keys(step_at):
         u = lax.rem(pair + step_at, 4)
         both = key_grads(1, u).astype(BF)
         dkv[2 * u] = both[:, :ROWS]
         dkv[2 * u + 1] = both[:, ROWS:]
         crossing(u).start()
-    for step_at in (2, 1, 3, 0):
+
+    def own_keys(step_at):
         u = lax.rem(pair + step_at, 4)
         both = key_grads(0, u)
         crossing(u).wait_recv()
@@ -484,8 +499,16 @@
             send_grad(2 * u + 1, kvo, 12).start()
         else:
             send_grad(mate, kvo, 12).start()
-        if step_at == XAT:
-            x_done()
+
+    other_keys(2)
+    other_keys(1)
+    own_keys(2)
+    x_done()
+    other_keys(3)
+    own_keys(1)
+    other_keys(0)
+    own_keys(3)
+    own_keys(0)
 
     recv4[y] = send4[y]
 
@@ -509,13 +532,22 @@
                 [piece[0:16], piece[16:32], piece[32:48]], axis=1
             )
 
-    for t in range(16):
-
-        @pl.when(active & (p != t))
-        def _():
-            remote(
-                ysend.at[t], yrecv.at[y], snd.at[15], rcv.at[7], patch_0=t // 2, patch_1=t % 2
-            ).start()
+    @pl.when(active)
+    def _():
+        for i in FAR + (0,):
+            for c in range(2):
+                if i == 0 and c == 1:
+                    continue
+                to = lax.rem(y + i, 8)
+                core = c if i else other
+                remote(
+                    ysend.at[2 * to + core],
+                    yrecv.at[y],
+                    snd.at[15],
+                    rcv.at[7],
+                    patch_0=to,
+                    patch_1=core,
+                ).start()
 
     @pl.when(active)
     def _():
@@ -569,6 +601,7 @@
     drain(send1.at[seven, qk], 0)
     drain(send1.at[seven, vo], 1)
     drain(send1.at[:, ko], 2)
+    drain(ktok.at[pl.ds(0, 8 * ROWS)], 16)
     drain(send1.at[:, vo], 3)
     drain(send2.at[seven, head], 4)
     drain(pa_s.at[0], 5)
@@ -649,7 +682,7 @@
         pltpu.VMEM((4, 8, 256), F32),
         pltpu.VMEM((4, PAD, 256), F32),
     ]
-    sems = [6, 16, 13, 8, 8, 8, 8, 8, 4, 6, 6]
+    sems = [6, 17, 13, 8, 8, 8, 8, 4, 6, 6]
     vmem = pl.BlockSpec(memory_space=pltpu.VMEM)
     hbm = pl.BlockSpec(memory_space=pltpu.HBM)
     wide = jax.ShapeDtypeStruct((1, FEAT, ROWS), F32)

time: 68.3 us -> 67.5 us (0.988)
  Pallas kernels: 66.9 us -> 66 us
    pallas_call x1, Pallas kernels: 65.3 us -> 64.4 us  [step(): pl.pallas_call(functools.partial(body, nx, nz), out_shape=results, in_spe...]
where the time goes in v6:
time: 67.5 us; the launch traced here: 67.3 us
  Pallas kernels  66 us (98%)
  between operations  1.29 us (2%)
    pallas_call x1, Pallas kernels, step(): pl.pallas_call(functools.partial(body, nx, nz), out_shape=results, in_spe...  64.4 us
    pallas_call x1, Pallas kernels, step(): pl.pallas_call(write_out, out_shape=results, in_specs=[pl.BlockSpec(memor...  1.59 us

profile of v6, /device:TPU:1, one launch (start us, length us, event | category | flops | bytes accessed | tf_op | source)
XLA Modules:
  0.0 67.3 jit_solution(10824244845379233202)
XLA Ops:
  1.3 64.4 %shard_map.110 = (f32[1,576,128]{2,1,0:T(8,128)S(1)}, f32[1,576,128]{2,1,0:T(8,128)S(1)}, f32[1,576,128]{2,1,0:T(8,128)S(1)}, f32[36,36]{1,0:T(8,128)S(1)}, f32[1,1]{1,0:T(1,128)}) custom-call(bf16[1,576,128]{2,1,0:T(8,128)(2,1)} %bitcast.7, bf16[1,576,128]{2,1,0:T(8,128)(2,1)} %bitcast.8, bf16[1,576,128]{2,1,0:T(8,128)(2,1)} %bitcast.9, s32[1,128]{1,0:T(1,128)} %seg_hbm.1, ...), custom_call_target="tpu_custom_call" | custom-call | tf_op jit(solution)/shard_map/pallas_call | solution.py:697
  65.7 1.6 %shard_map.111 = (f32[1,576,128]{2,1,0:T(8,128)}, f32[1,576,128]{2,1,0:T(8,128)}, f32[1,576,128]{2,1,0:T(8,128)}, f32[36,36]{1,0:T(8,128)}, f32[1,1]{1,0:T(1,128)}) custom-call(f32[1,576,128]{2,1,0:T(8,128)S(1)} %get-tuple-element.15.refs_0_, f32[1,576,128]{2,1,0:T(8,128)S(1)} %get-tuple-element.16.refs_1_, f32[1,576,128]{2,1,0:T(8,128)S(1)} %get-tuple-element.17.refs_2_, ...), custom_call_target="tpu_custom_call" | custom-call | tf_op jit(solution)/shard_map/pallas_call | solution.py:715

commit v7 on v6

--- a/solution.py
+++ b/solution.py
@@ -57,7 +57,7 @@
     dtok,
     p_s,
     ds_s,
-    rinv_s,
+    w_half,
     send2,
     recv2,
     at_s,
@@ -79,7 +79,7 @@
     ysend,
     yrecv,
     stat_s,
-    s_s,
+    qf_s,
     top_s,
     acc_s,
     load_sem,
@@ -136,31 +136,29 @@
 
     row = lax.broadcasted_iota(jnp.int32, (8, ROWS), 0)
     lane = lax.broadcasted_iota(jnp.int32, (8, ROWS), 1)
+    for c in loads[:4]:
+        c.wait()
     length = len_ref[0]
     live_t = p * ROWS + lane < length
-    for c in loads[:4]:
-        c.wait()
     code = jnp.where(live_t, jnp.broadcast_to(seg_s[...], (8, ROWS)), 8)
     low = jnp.bitwise_and(row, 3)
     weight = jnp.where(low == 0, 1, jnp.where(low == 1, 2, jnp.where(low == 2, 4, 8)))
     bit = jnp.where(jnp.bitwise_and(code, weight) != 0, 1.0, 0.0).astype(F32)
     mine = jnp.where(row < 4, bit, 1.0 - bit)
     q_mask = -MASK * mine
-    k_mask = MASK * (1.0 - mine)
-    v_ones = jnp.where(row == 0, 1.0, 0.0).astype(F32)
-    for at, (ref, extra) in enumerate(((q_s, q_mask), (k_s, k_mask), (v_s, v_ones))):
-        whole = ref[0].astype(F32)
-        for h in range(HEADS):
-            block = jnp.concatenate([whole[HEAD_DIM * h : HEAD_DIM * (h + 1)], extra], axis=0)
-            send1[h, PAD * at : PAD * (at + 1), :] = block.astype(BF)
+    parts = [ref[0].astype(F32) for ref in (k_s, q_s, v_s)]
+    for h in range(HEADS):
+        keys, asks, vals = [a[HEAD_DIM * h : HEAD_DIM * (h + 1)] for a in parts]
+        send1[h] = jnp.concatenate([keys, asks, q_mask, vals], axis=0).astype(BF)
     recv1[0, y] = send1[y]
 
     recv3[...] = jnp.zeros_like(recv3)
     pl.semaphore_wait(barrier, 15 + (nx - 1) + (nz - 1))
 
-    qk = pl.ds(0, 2 * PAD)
-    ko = pl.ds(PAD, PAD)
-    vo = pl.ds(2 * PAD, PAD)
+    qk = pl.ds(0, 2 * HEAD_DIM + 8)
+    ko = pl.ds(0, HEAD_DIM)
+    vo = pl.ds(2 * HEAD_DIM + 8, HEAD_DIM)
+    mo = pl.ds(2 * HEAD_DIM, PAD)
 
     def spread(rows, n, rsem):
         for i in FAR:
@@ -188,9 +186,15 @@
             patch_1=other,
         )
 
-    def token_major(dst, c, src, part):
-        at = pl.ds(pl.multiple_of((8 * c + src) * ROWS, ROWS), ROWS)
-        dst[at, :] = recv1[c, src, PAD * part : PAD * (part + 1), :].astype(F32).T.astype(BF)
+    def row_block(src, c=0):
+        return pl.ds(pl.multiple_of((8 * c + src) * ROWS, ROWS), ROWS)
+
+    def take(src):
+        asks = recv1[0, src, HEAD_DIM : 2 * HEAD_DIM + 8, :].astype(F32)
+        qf_s[src] = asks.astype(BF)
+        keys = recv1[0, src, 0:HEAD_DIM, :].astype(F32)
+        keys = jnp.concatenate([keys, MASK + asks[HEAD_DIM:]], axis=0)
+        ktok[row_block(src), :] = keys.T.astype(BF)
 
     def pass_keys(i):
         at = pl.multiple_of(source(i) * ROWS, ROWS)
@@ -203,14 +207,14 @@
         )
 
     passed = [pass_on(i, ko, 2, rcv.at[8]) for i in range(8)]
-    passed_v = [pass_on(i, vo, 3, rcv.at[9]) for i in range(8)]
-    token_major(ktok, 0, y, 1)
+    passed_v = [pass_on(i, mo, 3, rcv.at[9]) for i in range(8)]
+    take(y)
     pass_keys(0).start()
     passed[0].start()
     passed_v[0].start()
     for i in NEAR:
         block_in(i, qk, r1)
-        token_major(ktok, 0, source(i), 1)
+        take(source(i))
         pass_keys(i).start()
         passed[i].start()
 
@@ -220,12 +224,16 @@
     half = 8 * ROWS
 
     def queries(j):
-        return jnp.concatenate([recv1[0, 2 * j, 0:PAD, :], recv1[0, 2 * j + 1, 0:PAD, :]], axis=1)
+        return jnp.concatenate([qf_s[2 * j], qf_s[2 * j + 1]], axis=1)
+
+    def forward_half(j, c):
+        scores = dot(ktok[half * c : half * (c + 1), :], queries(j), 1, 0)
+        top = jnp.max(scores, axis=0, keepdims=True)
+        p_s[j, half * c : half * (c + 1), :] = jnp.exp2((scores - top) * factor).astype(BF)
+        return top
 
     def forward_own(j, carry):
-        scores = dot(ktok[0:half, :], queries(j), 1, 0)
-        s_s[j] = scores
-        top_s[j] = jnp.broadcast_to(jnp.max(scores, axis=0, keepdims=True), (8, 2 * ROWS))
+        top_s[j] = jnp.broadcast_to(forward_half(j, 0), (8, 2 * ROWS))
         return carry
 
     lax.fori_loop(0, 4, forward_own, 0)
@@ -233,10 +241,11 @@
         pass_keys(i).wait_recv()
 
     def forward_other(j, carry):
-        scores = dot(ktok[half : 2 * half, :], queries(j), 1, 0)
-        top = jnp.maximum(top_s[j, 0:1, :], jnp.max(scores, axis=0, keepdims=True))
-        p_s[j, half : 2 * half, :] = jnp.exp2((scores - top) * factor).astype(BF)
-        p_s[j, 0:half, :] = jnp.exp2((s_s[j] - top) * factor).astype(BF)
+        top = forward_half(j, 1)
+        mine = top_s[j, 0:1, :]
+        best = jnp.maximum(mine, top)
+        for c, one in enumerate((mine, top)):
+            w_half[c, j] = jnp.broadcast_to(jnp.exp2((one - best) * factor), (8, 2 * ROWS))
         return carry
 
     lax.fori_loop(0, 4, forward_other, 0)
@@ -244,20 +253,21 @@
         block_in(i, vo, r1v)
         passed_v[i].start()
 
-    def lanes(c, part):
-        return jnp.concatenate(
-            [recv1[c, src, PAD * part : PAD * (part + 1), :] for src in range(8)], axis=1
-        )
+    def lanes(c, start, end):
+        return jnp.concatenate([recv1[c, src, start:end, :] for src in range(8)], axis=1)
+
+    def values(c):
+        return lanes(c, 2 * HEAD_DIM, 3 * HEAD_DIM + 8)
 
     def values_own(j, carry):
-        acc_s[j] = dot(lanes(0, 2), p_s[j, 0:half, :], 1, 0)
+        acc_s[j] = dot(values(0), p_s[j, 0:half, :], 1, 0)
         return carry
 
     lax.fori_loop(0, 4, values_own, 0)
-    crossed = recv1.at[1, :, vo]
+    crossed = recv1.at[1, :, mo]
     remote(crossed, crossed, snd.at[3], rcv.at[9], patch_0=y).wait_recv()
 
-    head = pl.ds(0, HEAD_DIM)
+    head = pl.ds(8, HEAD_DIM)
 
     def send_attn(s):
         return remote(
@@ -266,9 +276,11 @@
 
     for step_at in (2, 1, 3, 0):
         j = lax.rem(pair + step_at, 4)
-        accum = acc_s[j] + dot(lanes(1, 2), p_s[j, half : 2 * half, :], 1, 0)
-        rinv = 1.0 / accum[HEAD_DIM : HEAD_DIM + 1, :]
-        rinv_s[j] = jnp.broadcast_to(rinv, (8, 2 * ROWS))
+        mine, yours = w_half[0, j, 0:1, :], w_half[1, j, 0:1, :]
+        accum = acc_s[j] * mine + dot(values(1), p_s[j, half : 2 * half, :], 1, 0) * yours
+        rinv = -MASK / (accum[0:1, :] + accum[4:5, :])
+        w_half[0, j] = jnp.broadcast_to(mine * rinv, (8, 2 * ROWS))
+        w_half[1, j] = jnp.broadcast_to(yours * rinv, (8, 2 * ROWS))
         attn = (accum * rinv).astype(BF)
         send2[2 * j] = attn[:, :ROWS]
         send2[2 * j + 1] = attn[:, ROWS:]
@@ -280,9 +292,10 @@
     recv2[y] = send2[y]
 
     def backward_layouts(src, carry):
-        token_major(vtok, 0, src, 2)
-        token_major(vtok, 1, src, 2)
-        token_major(qtok, 0, src, 0)
+        for c in range(2):
+            vals = recv1[c, src, 2 * HEAD_DIM : 3 * HEAD_DIM + 8, :]
+            vtok[row_block(src, c), :] = vals.astype(F32).T.astype(BF)
+        qtok[row_block(src), :] = qf_s[src].astype(F32).T.astype(BF)
         return carry
 
     lax.fori_loop(0, 8, backward_layouts, 0)
@@ -294,7 +307,7 @@
         send2.at[seven, head], recv2.at[seven, head], snd.at[4], rcv.at[0], patch_0=y
     ).wait_recv()
     for h in range(HEADS):
-        at_s[HEAD_DIM * h : HEAD_DIM * (h + 1), :] = recv2[h].astype(F32)[:HEAD_DIM]
+        at_s[HEAD_DIM * h : HEAD_DIM * (h + 1), :] = recv2[h].astype(F32)[8:]
     attn_t = at_s[...].astype(BF)
     pa_s[0] = attn_t
     swap_a = remote(pa_s.at[0], pa_s.at[1], snd.at[5], rcv.at[1], patch_1=other)
@@ -315,7 +328,7 @@
     grad_attn = dot(w_s[...], grad_t, 1, 0)
     for h in range(HEADS):
         block = jnp.concatenate(
-            [grad_attn[HEAD_DIM * h : HEAD_DIM * (h + 1)], jnp.zeros((8, ROWS), F32)], axis=0
+            [jnp.zeros((8, ROWS), F32), grad_attn[HEAD_DIM * h : HEAD_DIM * (h + 1)]], axis=0
         )
         send3[h] = block.astype(BF)
     for i in FAR:
@@ -323,19 +336,20 @@
         remote(
             send3.at[to, head], recv3.at[y, head], snd.at[6], r3.at[i], patch_0=to
         ).start()
-    recv3[y, 0:HEAD_DIM, :] = send3[y, 0:HEAD_DIM, :]
+    recv3[y] = send3[y]
 
     swap_a.wait_recv()
     swap_g.wait_recv()
-    left = jnp.concatenate([g_s[k], pg_s[...]], axis=1)
     right = jnp.concatenate([pa_s[0], pa_s[1]], axis=1)
-    partial = dot(left, right, 1, 1)
-    for xx in range(nx):
-        chunk = partial[part * xx : part * (xx + 1)]
+
+    def x_chunk(xx):
+        at = pl.ds(pl.multiple_of(part * xx, 16), part)
+        chunk = dot(jnp.concatenate([g_s[k, at, :], pg_s[at, :]], axis=1), right, 1, 1)
         rest = jnp.concatenate([chunk[: part // 2, 512:], chunk[part // 2 :, 512:]], axis=1)
         for g in range(4):
             xsend[xx, part * g : part * (g + 1), :] = chunk[:, ROWS * g : ROWS * (g + 1)].astype(BF)
         xsend[xx, 4 * part :, :] = jnp.concatenate([rest, jnp.zeros((8, ROWS), F32)], axis=0).astype(BF)
+
     lo, hi = pl.ds(0, 336), pl.ds(336, 320)
     up, down, across = lax.rem(x + 1, 4), lax.rem(x + 3, 4), lax.rem(x + 2, 4)
     xring = [
@@ -346,8 +360,14 @@
         remote(xacc.at[lo], xin.at[0, lo], xs.at[4], xr.at[4], dp_0=up),
         remote(xacc.at[hi], xin.at[1, hi], xs.at[5], xr.at[5], dp_0=down),
     ]
-    for c in xring[:4]:
-        c.start()
+    x_chunk(across)
+    xring[0].start()
+    xring[1].start()
+    x_chunk(up)
+    xring[2].start()
+    x_chunk(down)
+    xring[3].start()
+    x_chunk(x)
 
     def x_relay():
         for n, (rows, size, to) in enumerate(((0, 336, up), (336, 320, down))):
@@ -411,16 +431,19 @@
         else:
             third_in(mate)
         grads = jnp.concatenate([recv3[2 * j], recv3[2 * j + 1]], axis=1).astype(F32)
-        folded = grads * rinv_s[j, 0:1, :]
-        dtok[pl.ds(pl.multiple_of(j * 2 * ROWS, 2 * ROWS), 2 * ROWS), :] = folded.T.astype(BF)
-        folded = folded.astype(BF)
-        attn = jnp.concatenate([send2[2 * j], send2[2 * j + 1]], axis=1)
-        delta = jnp.sum(folded.astype(F32) * attn.astype(F32), axis=0, keepdims=True)
-        dprobs = dot(vtok[...], folded, 1, 0)
-        dscores = (p_s[j].astype(F32) * (dprobs - delta)).astype(BF)
-        ds_s[j] = dscores
-        keys = jnp.concatenate([lanes(0, 1), lanes(1, 1)], axis=1)
-        dq = (dot(keys, dscores, 1, 0) * scale).astype(BF)
+        attn = jnp.concatenate([send2[2 * j], send2[2 * j + 1]], axis=1).astype(F32)
+        at = pl.ds(pl.multiple_of(j * 2 * ROWS, 2 * ROWS), 2 * ROWS)
+        for c in range(2):
+            folded = grads * w_half[c, j, 0:1, :]
+            dtok[c, at, :] = folded.T.astype(BF)
+            folded = folded.astype(BF)
+            delta = jnp.sum(folded.astype(F32) * attn, axis=0, keepdims=True)
+            these = slice(half * c, half * (c + 1))
+            dprobs = dot(vtok[these, :], folded, 1, 0)
+            ds_s[j, these, :] = (p_s[j, these, :].astype(F32) * (dprobs - delta)).astype(BF)
+        keys = jnp.concatenate([lanes(0, 0, HEAD_DIM), lanes(1, 0, HEAD_DIM)], axis=1)
+        dq = dot(keys, ds_s[j], 1, 0) * scale
+        dq = jnp.concatenate([dq, jnp.zeros((8, 2 * ROWS), F32)], axis=0).astype(BF)
         send4[2 * j, 0:PAD, :] = dq[:, :ROWS]
         send4[2 * j + 1, 0:PAD, :] = dq[:, ROWS:]
         if step_at:
@@ -443,8 +466,8 @@
         ds_rows = jnp.concatenate([ds_s[j, at, :] for j in range(4)], axis=1)
         p_rows = jnp.concatenate([p_s[j, at, :] for j in range(4)], axis=1)
         dk = (dot(ds_rows, qtok[...], 1, 0) * scale).T
-        dv = dot(p_rows, dtok[...], 1, 0).T
-        return jnp.concatenate([dk[:HEAD_DIM], dv[:HEAD_DIM]], axis=0)
+        dv = dot(p_rows, dtok[c], 1, 0).T
+        return jnp.concatenate([dk[:HEAD_DIM], dv[8:]], axis=0)
 
     cols = part // zh
     active = z // zh == k
@@ -602,7 +625,7 @@
     drain(send1.at[seven, vo], 1)
     drain(send1.at[:, ko], 2)
     drain(ktok.at[pl.ds(0, 8 * ROWS)], 16)
-    drain(send1.at[:, vo], 3)
+    drain(send1.at[:, mo], 3)
     drain(send2.at[seven, head], 4)
     drain(pa_s.at[0], 5)
     drain(send3.at[seven, head], 6)
@@ -648,15 +671,15 @@
         pltpu.VMEM((1, ROWS), jnp.int32),
         pltpu.VMEM((FEAT, WIDTH), BF),
         pltpu.VMEM((1, ROWS, WIDTH), BF),
-        pltpu.VMEM((8, 3 * PAD, ROWS), BF),
-        pltpu.VMEM((2, 8, 3 * PAD, ROWS), BF),
+        pltpu.VMEM((8, 3 * HEAD_DIM + 8, ROWS), BF),
+        pltpu.VMEM((2, 8, 3 * HEAD_DIM + 8, ROWS), BF),
         pltpu.VMEM((2048, PAD), BF),
         pltpu.VMEM((2048, PAD), BF),
         pltpu.VMEM((1024, PAD), BF),
-        pltpu.VMEM((1024, PAD), BF),
+        pltpu.VMEM((2, 1024, PAD), BF),
         pltpu.VMEM((4, 2048, 256), BF),
         pltpu.VMEM((4, 2048, 256), BF),
-        pltpu.VMEM((4, 8, 256), F32),
+        pltpu.VMEM((2, 4, 8, 256), F32),
         pltpu.VMEM((8, PAD, ROWS), BF),
         pltpu.VMEM((8, PAD, ROWS), BF),
         pltpu.VMEM((FEAT, ROWS), F32),
@@ -678,7 +701,7 @@
         pltpu.VMEM((16, 16, 128), F32),
         pltpu.VMEM((8, 16, 128), F32),
         pltpu.VMEM((19 + nx + nz, 8, ROWS), F32),
-        pltpu.VMEM((4, 1024, 256), F32),
+        pltpu.VMEM((8, PAD, ROWS), BF),
         pltpu.VMEM((4, 8, 256), F32),
         pltpu.VMEM((4, PAD, 256), F32),
     ]

time: 67.5 us -> 66.6 us (0.987)
  Pallas kernels: 66 us -> 65.2 us
    pallas_call x1, Pallas kernels: 64.4 us -> 63.6 us  [step(): pl.pallas_call(functools.partial(body, nx, nz), out_shape=results, in_spe...]
where the time goes in v7:
time: 66.6 us; the launch traced here: 66.5 us
  Pallas kernels  65.2 us (98%)
  between operations  1.29 us (2%)
    pallas_call x1, Pallas kernels, step(): pl.pallas_call(functools.partial(body, nx, nz), out_shape=results, in_spe...  63.6 us
    pallas_call x1, Pallas kernels, step(): pl.pallas_call(write_out, out_shape=results, in_specs=[pl.BlockSpec(memor...  1.59 us

profile of v7, /device:TPU:1, one launch (start us, length us, event | category | flops | bytes accessed | tf_op | source)
XLA Modules:
  0.0 66.5 jit_solution(5609214896050279609)
XLA Ops:
  1.3 63.6 %shard_map.110 = (f32[1,576,128]{2,1,0:T(8,128)S(1)}, f32[1,576,128]{2,1,0:T(8,128)S(1)}, f32[1,576,128]{2,1,0:T(8,128)S(1)}, f32[36,36]{1,0:T(8,128)S(1)}, f32[1,1]{1,0:T(1,128)}) custom-call(bf16[1,576,128]{2,1,0:T(8,128)(2,1)} %bitcast.7, bf16[1,576,128]{2,1,0:T(8,128)(2,1)} %bitcast.8, bf16[1,576,128]{2,1,0:T(8,128)(2,1)} %bitcast.9, s32[1,128]{1,0:T(1,128)} %seg_hbm.1, ...), custom_call_target="tpu_custom_call" | custom-call | tf_op jit(solution)/shard_map/pallas_call | solution.py:720
  64.9 1.6 %shard_map.111 = (f32[1,576,128]{2,1,0:T(8,128)}, f32[1,576,128]{2,1,0:T(8,128)}, f32[1,576,128]{2,1,0:T(8,128)}, f32[36,36]{1,0:T(8,128)}, f32[1,1]{1,0:T(1,128)}) custom-call(f32[1,576,128]{2,1,0:T(8,128)S(1)} %get-tuple-element.15.refs_0_, f32[1,576,128]{2,1,0:T(8,128)S(1)} %get-tuple-element.16.refs_1_, f32[1,576,128]{2,1,0:T(8,128)S(1)} %get-tuple-element.17.refs_2_, ...), custom_call_target="tpu_custom_call" | custom-call | tf_op jit(solution)/shard_map/pallas_call | solution.py:738

commit v8 on v7

--- a/solution.py
+++ b/solution.py
@@ -49,6 +49,8 @@
     seg_s,
     w_s,
     t_s,
+    wt_s,
+    tt_s,
     send1,
     recv1,
     ktok,
@@ -212,6 +214,17 @@
     pass_keys(0).start()
     passed[0].start()
     passed_v[0].start()
+
+    loads[4].wait()
+    loads[5].wait()
+
+    def turn(c, carry):
+        at = pl.ds(pl.multiple_of(c * ROWS, ROWS), ROWS)
+        wt_s[at, :] = w_s[:, at].astype(F32).T.astype(BF)
+        tt_s[at, :] = t_s[0, :, at].astype(F32).T
+        return carry
+
+    lax.fori_loop(0, WIDTH // ROWS, turn, 0)
     for i in NEAR:
         block_in(i, qk, r1)
         take(source(i))
@@ -300,8 +313,6 @@
 
     lax.fori_loop(0, 8, backward_layouts, 0)
 
-    loads[4].wait()
-    loads[5].wait()
     seven = pl.ds(0, 7)
     remote(
         send2.at[seven, head], recv2.at[seven, head], snd.at[4], rcv.at[0], patch_0=y
@@ -312,12 +323,11 @@
     pa_s[0] = attn_t
     swap_a = remote(pa_s.at[0], pa_s.at[1], snd.at[5], rcv.at[1], patch_1=other)
     swap_a.start()
-    output = dot(attn_t, w_s[...], 0, 0)
-    token = lax.broadcasted_iota(jnp.int32, (ROWS, WIDTH), 0)
+    output = dot(wt_s[...], attn_t, 1, 0)
+    token = lax.broadcasted_iota(jnp.int32, (WIDTH, ROWS), 1)
     live = p * ROWS + token < length
-    error = jnp.where(live, output - t_s[0].astype(F32), 0.0)
-    grad_out = (2.0 * error).astype(BF)
-    grad_t = (2.0 * error).T.astype(BF)
+    error = jnp.where(live, output - tt_s[...], 0.0)
+    grad_t = (2.0 * error).astype(BF)
     part = WIDTH // (2 * nx)
     for zhalf in range(2):
         for xx in range(nx):
@@ -671,6 +681,8 @@
         pltpu.VMEM((1, ROWS), jnp.int32),
         pltpu.VMEM((FEAT, WIDTH), BF),
         pltpu.VMEM((1, ROWS, WIDTH), BF),
+        pltpu.VMEM((WIDTH, FEAT), BF),
+        pltpu.VMEM((WIDTH, ROWS), F32),
         pltpu.VMEM((8, 3 * HEAD_DIM + 8, ROWS), BF),
         pltpu.VMEM((2, 8, 3 * HEAD_DIM + 8, ROWS), BF),
         pltpu.VMEM((2048, PAD), BF),

time: 66.6 us -> 66.8 us (level)
  no operation moved by 1% of the time
where the time goes in v8:
time: 66.8 us; the launch traced here: 66.6 us
  Pallas kernels  65.4 us (98%)
  between operations  1.29 us (2%)
    pallas_call x1, Pallas kernels, step(): pl.pallas_call(functools.partial(body, nx, nz), out_shape=results, in_spe...  63.8 us
    pallas_call x1, Pallas kernels, step(): pl.pallas_call(write_out, out_shape=results, in_specs=[pl.BlockSpec(memor...  1.59 us

profile of v8, /device:TPU:1, one launch (start us, length us, event | category | flops | bytes accessed | tf_op | source)
XLA Modules:
  0.0 66.6 jit_solution(3934412570108266784)
XLA Ops:
  1.3 63.8 %shard_map.110 = (f32[1,576,128]{2,1,0:T(8,128)S(1)}, f32[1,576,128]{2,1,0:T(8,128)S(1)}, f32[1,576,128]{2,1,0:T(8,128)S(1)}, f32[36,36]{1,0:T(8,128)S(1)}, f32[1,1]{1,0:T(1,128)}) custom-call(bf16[1,576,128]{2,1,0:T(8,128)(2,1)} %bitcast.7, bf16[1,576,128]{2,1,0:T(8,128)(2,1)} %bitcast.8, bf16[1,576,128]{2,1,0:T(8,128)(2,1)} %bitcast.9, s32[1,128]{1,0:T(1,128)} %seg_hbm.1, ...), custom_call_target="tpu_custom_call" | custom-call | tf_op jit(solution)/shard_map/pallas_call | solution.py:732
  65.1 1.6 %shard_map.111 = (f32[1,576,128]{2,1,0:T(8,128)}, f32[1,576,128]{2,1,0:T(8,128)}, f32[1,576,128]{2,1,0:T(8,128)}, f32[36,36]{1,0:T(8,128)}, f32[1,1]{1,0:T(1,128)}) custom-call(f32[1,576,128]{2,1,0:T(8,128)S(1)} %get-tuple-element.15.refs_0_, f32[1,576,128]{2,1,0:T(8,128)S(1)} %get-tuple-element.16.refs_1_, f32[1,576,128]{2,1,0:T(8,128)S(1)} %get-tuple-element.17.refs_2_, ...), custom_call_target="tpu_custom_call" | custom-call | tf_op jit(solution)/shard_map/pallas_call | solution.py:750

commit v9 on v7

--- a/solution.py
+++ b/solution.py
@@ -451,7 +451,7 @@
             send_grad(2 * j + 1, qo, 11).start()
         else:
             send_grad(mate, qo, 11).start()
-        if step_at == 1:
+        if step_at == 0:
             x_relay()
 
     stat_s[1] = stat_sum(0, 3, 16)
@@ -473,8 +473,6 @@
     active = z // zh == k
 
     def x_done():
-        stat_s[2] = stat_sum(1, 19, nx)
-        stat_send(2, 19 + nx, nz, z, lambda t: {"dp_1": t})
         for c in xring[2:]:
             c.wait_recv()
         total = xsend[x].astype(F32) + xin[0].astype(F32) + xin[1].astype(F32)
@@ -523,10 +521,12 @@
         else:
             send_grad(mate, kvo, 12).start()
 
+    x_done()
     other_keys(2)
     other_keys(1)
     own_keys(2)
-    x_done()
+    stat_s[2] = stat_sum(1, 19, nx)
+    stat_send(2, 19 + nx, nz, z, lambda t: {"dp_1": t})
     other_keys(3)
     own_keys(1)
     other_keys(0)

time: 66.6 us -> 64.8 us (0.973)
  Pallas kernels: 65.2 us -> 63.3 us
    pallas_call x1, Pallas kernels: 63.6 us -> 61.7 us  [step(): pl.pallas_call(functools.partial(body, nx, nz), out_shape=results, in_spe...]
where the time goes in v9:
time: 64.8 us; the launch traced here: 64.6 us
  Pallas kernels  63.3 us (98%)
  between operations  1.29 us (2%)
    pallas_call x1, Pallas kernels, step(): pl.pallas_call(functools.partial(body, nx, nz), out_shape=results, in_spe...  61.7 us
    pallas_call x1, Pallas kernels, step(): pl.pallas_call(write_out, out_shape=results, in_specs=[pl.BlockSpec(memor...  1.59 us

profile of v9, /device:TPU:1, one launch (start us, length us, event | category | flops | bytes accessed | tf_op | source)
XLA Modules:
  0.0 64.6 jit_solution(14293222255736096565)
XLA Ops:
  1.3 61.7 %shard_map.110 = (f32[1,576,128]{2,1,0:T(8,128)S(1)}, f32[1,576,128]{2,1,0:T(8,128)S(1)}, f32[1,576,128]{2,1,0:T(8,128)S(1)}, f32[36,36]{1,0:T(8,128)S(1)}, f32[1,1]{1,0:T(1,128)}) custom-call(bf16[1,576,128]{2,1,0:T(8,128)(2,1)} %bitcast.7, bf16[1,576,128]{2,1,0:T(8,128)(2,1)} %bitcast.8, bf16[1,576,128]{2,1,0:T(8,128)(2,1)} %bitcast.9, s32[1,128]{1,0:T(1,128)} %seg_hbm.1, ...), custom_call_target="tpu_custom_call" | custom-call | tf_op jit(solution)/shard_map/pallas_call | solution.py:720
  63.0 1.6 %shard_map.111 = (f32[1,576,128]{2,1,0:T(8,128)}, f32[1,576,128]{2,1,0:T(8,128)}, f32[1,576,128]{2,1,0:T(8,128)}, f32[36,36]{1,0:T(8,128)}, f32[1,1]{1,0:T(1,128)}) custom-call(f32[1,576,128]{2,1,0:T(8,128)S(1)} %get-tuple-element.15.refs_0_, f32[1,576,128]{2,1,0:T(8,128)S(1)} %get-tuple-element.16.refs_1_, f32[1,576,128]{2,1,0:T(8,128)S(1)} %get-tuple-element.17.refs_2_, ...), custom_call_target="tpu_custom_call" | custom-call | tf_op jit(solution)/shard_map/pallas_call | solution.py:738

commit v10 on v9

--- a/solution.py
+++ b/solution.py
@@ -423,6 +423,7 @@
             send3.at[y, head], recv3.at[s, head], snd.at[6], r3.at[i], patch_0=y
         ).wait_recv()
 
+    x_relay()
     for step_at in (0, 1, 3, 2):
         j = lax.rem(pair + step_at, 4)
         if step_at:
@@ -451,8 +452,6 @@
             send_grad(2 * j + 1, qo, 11).start()
         else:
             send_grad(mate, qo, 11).start()
-        if step_at == 0:
-            x_relay()
 
     stat_s[1] = stat_sum(0, 3, 16)
     stat_send(1, 19, nx, x, lambda t: {"dp_0": t})

time: 64.8 us -> 63.8 us (0.985)
  Pallas kernels: 63.3 us -> 62.4 us
    pallas_call x1, Pallas kernels: 61.7 us -> 60.8 us  [step(): pl.pallas_call(functools.partial(body, nx, nz), out_shape=results, in_spe...]
where the time goes in v10:
time: 63.8 us; the launch traced here: 63.7 us
  Pallas kernels  62.4 us (98%)
  between operations  1.29 us (2%)
    pallas_call x1, Pallas kernels, step(): pl.pallas_call(functools.partial(body, nx, nz), out_shape=results, in_spe...  60.8 us
    pallas_call x1, Pallas kernels, step(): pl.pallas_call(write_out, out_shape=results, in_specs=[pl.BlockSpec(memor...  1.59 us

profile of v10, /device:TPU:1, one launch (start us, length us, event | category | flops | bytes accessed | tf_op | source)
XLA Modules:
  0.0 63.7 jit_solution(8695472356352830877)
XLA Ops:
  1.3 60.8 %shard_map.110 = (f32[1,576,128]{2,1,0:T(8,128)S(1)}, f32[1,576,128]{2,1,0:T(8,128)S(1)}, f32[1,576,128]{2,1,0:T(8,128)S(1)}, f32[36,36]{1,0:T(8,128)S(1)}, f32[1,1]{1,0:T(1,128)}) custom-call(bf16[1,576,128]{2,1,0:T(8,128)(2,1)} %bitcast.7, bf16[1,576,128]{2,1,0:T(8,128)(2,1)} %bitcast.8, bf16[1,576,128]{2,1,0:T(8,128)(2,1)} %bitcast.9, s32[1,128]{1,0:T(1,128)} %seg_hbm.1, ...), custom_call_target="tpu_custom_call" | custom-call | tf_op jit(solution)/shard_map/pallas_call | solution.py:719
  62.1 1.6 %shard_map.111 = (f32[1,576,128]{2,1,0:T(8,128)}, f32[1,576,128]{2,1,0:T(8,128)}, f32[1,576,128]{2,1,0:T(8,128)}, f32[36,36]{1,0:T(8,128)}, f32[1,1]{1,0:T(1,128)}) custom-call(f32[1,576,128]{2,1,0:T(8,128)S(1)} %get-tuple-element.15.refs_0_, f32[1,576,128]{2,1,0:T(8,128)S(1)} %get-tuple-element.16.refs_1_, f32[1,576,128]{2,1,0:T(8,128)S(1)} %get-tuple-element.17.refs_2_, ...), custom_call_target="tpu_custom_call" | custom-call | tf_op jit(solution)/shard_map/pallas_call | solution.py:737
